TPU v7x, 32 devices: a whole 2x2x4 slice. The times are simulated.
32 devices in a mesh: grp: 2 (over y), vec: 4 (over z), walk: 2 (over x), orb: 2 (over core).
Axes of the slice: x: 2, y: 2, z: 4, core: 2. Of those that a mesh axis runs over, the one named last changes fastest.
Arguments:
- walkers: bfloat16 [32, 512, 128], P(('grp', 'walk'), 'orb'), parts along dimension 0, may hold values from -3 to 3
- inv_intersection: bfloat16 [32, 128, 128], P(('grp', 'walk')), parts along dimension 0, may hold values from -0.5 to 0.5
- trial: bfloat16 [512, 128], replicated, may hold values from -0.25 to 0.25
- vectors: bfloat16 [32, 512, 512], P('vec', 'orb')
- aux_field: float32 [32, 32], P(('grp', 'walk'), 'vec'), parts along dimension 0, may hold values from -5 to 5
- log_weight: float32 [32], P(('grp', 'walk')), parts along dimension 0, may hold values from -4 to 4
- copy_list: int32 [32], P(('grp', 'walk')), parts along dimension 0, may hold values from 0 to 15
Outputs:
- walkers_out: bfloat16 [32, 512, 128], P(('grp', 'walk'), 'orb'), parts along dimension 0
- weights_out: float32 [32], P(('grp', 'walk')), parts along dimension 0
There are 2 independent parts, one for each index of `grp`. A program takes and returns all parts, laid end to end along the dimension named above; an argument that names none is the same for every part. Nothing has to cross between parts.
Inputs may be any that keep to these rules, and one draw needn't show every extreme that they name: `copy_list`: the walker, within the same ensemble, whose copy fills the slot.
All inputs are finite; a program needn't handle non-finite values.
Results may differ from a plain program's by a relative error of at most 0.008.
Values may be sent and summed in bfloat16 or wider, within the bound.
A program may use at most 64 MiB of HBM per device.

v0:
```python
import functools
import math

import jax
import jax.numpy as jnp
from jax import lax
from jax.experimental import pallas as pl
from jax.experimental.pallas import tpu as pltpu
from jax.sharding import PartitionSpec as P

ORDER = 6
PIECES = 4
SKEW = 4
PARTS = 2
MESH = pl.DeviceIdType.MESH
F32 = jnp.float32
BF16 = jnp.bfloat16

step_root = math.sqrt(0.08)


def remote(src, dst, send, recv, where):
    return pltpu.make_async_remote_copy(
        src_ref=src, dst_ref=dst, send_sem=send, recv_sem=recv, device_id=where, device_id_type=MESH
    )


def kernel(
    depth, width,
    walkers, inverse, trial, vectors, aux, log_weight, copy_list,
    out, out_log,
    green, mixed, bias_own, bias_in, other_rows, partial, arrived, leaving, crossed, given, operator, full, term, result, every,
    factor_in, factor_out, logs,
    bias_sems, rows_sems, chain_send, chain_recv, factor_send, factor_recv, swap_send, swap_recv, cross_recv,
    every_recv, own_sends, next_send, across_send, log_send, log_recv,
):
    z = lax.axis_index("vec")
    x = lax.axis_index("walk")
    o = lax.axis_index("orb")
    last = depth - 1
    local, rows, electrons = walkers.shape
    count, _, orbitals = vectors.shape
    half = local // 2
    block = orbitals // 4
    span = 2 * block // count
    wide = count * span
    packed = partial.shape[1]
    piece = packed // PIECES
    chunks = half * PIECES
    mine = half // 2

    barrier = pltpu.get_barrier_semaphore()

    def greet(where):
        pl.semaphore_signal(barrier, inc=1, device_id=where, device_id_type=MESH)

    greet({"orb": 1 - o})
    for hop in range(1, width):
        for core in range(2):
            greet({"walk": lax.rem(x + hop, width), "orb": core})

    @pl.when(z > 0)
    def _():
        for core in range(2):
            greet({"vec": z - 1, "orb": core})

    @pl.when(z < last)
    def _():
        for core in range(2):
            greet({"vec": z + 1, "orb": core})

    for w in range(local):
        green[w] = jnp.dot(walkers[w], inverse[w], preferred_element_type=F32).astype(BF16)
    for g in range(count):
        mixed[g] = jnp.dot(vectors[g], trial[...], preferred_element_type=F32).astype(BF16)
    gram = jnp.zeros((local * span, wide), F32)
    for j in range(rows // span):
        left = green[:, j * span:(j + 1) * span, :].reshape(local * span, electrons)
        right = mixed[:, j * span:(j + 1) * span, :].reshape(wide, electrons)
        gram = gram + lax.dot_general(left, right, (((1,), (1,)), ((), ())), preferred_element_type=F32)
    row_id = lax.broadcasted_iota(jnp.int32, (local * span, wide), 0)
    col_id = lax.broadcasted_iota(jnp.int32, (local * span, wide), 1)
    same = row_id % span == col_id % span
    folded = jnp.sum(jnp.where(same, gram, 0.0).reshape(local, span, wide), axis=1)
    wide_row = lax.broadcasted_iota(jnp.int32, (wide, wide), 0)
    wide_col = lax.broadcasted_iota(jnp.int32, (wide, wide), 1)
    groups = jnp.where(wide_row // span == wide_col // span, 1.0, 0.0).astype(F32)
    bias_own[...] = jnp.dot(folded, groups, precision=lax.Precision.HIGHEST, preferred_element_type=F32)
    pick_row = lax.broadcasted_iota(jnp.int32, (count, wide), 0)
    pick_col = lax.broadcasted_iota(jnp.int32, (count, wide), 1)
    pick = jnp.where(pick_row == pick_col // span, 1.0, 0.0).astype(F32)
    drawn = jnp.dot(aux[...], pick, precision=lax.Precision.HIGHEST, preferred_element_type=F32)
    sides = jnp.where(z > 0, 2, 0) + jnp.where(z < last, 2, 0)
    pl.semaphore_wait(barrier, 1 + 2 * (width - 1) + sides)

    rows_copy = remote(walkers, other_rows, rows_sems.at[0], rows_sems.at[1], {"orb": 1 - o})
    rows_copy.start()

    bias_copy = remote(bias_own, bias_in, bias_sems.at[0], bias_sems.at[1], {"orb": 1 - o})
    bias_copy.start()
    bias_copy.wait()
    bias = bias_own[...] + bias_in[...]
    shift = -step_root * bias
    field = drawn - shift
    factor = jnp.sum(drawn * shift - 0.5 * shift * shift, axis=1, keepdims=True) * (1.0 / span)
    factor = jnp.broadcast_to(factor, (local, logs.shape[2]))
    weighted = (field * step_root).astype(BF16).astype(F32)
    spread = jnp.broadcast_to(weighted[:, None, :], (local, span, wide)).reshape(local * span, wide)
    kron = jnp.where(same, spread, 0.0).astype(BF16)

    for j in range(block // span):
        here = slice(j * span, (j + 1) * span)
        cols = pl.ds(pl.multiple_of(o * block, block), 3 * block)
        strip = vectors[:, here, cols].reshape(wide, 3 * block)
        summed = jnp.dot(kron, strip, preferred_element_type=F32)
        for slot in range(3):
            partial[:, slot * block + j * span:slot * block + (j + 1) * span, :] = summed[
                :, slot * block:(slot + 1) * block
            ].reshape(local, span, block)
        below = slice(block + j * span, block + (j + 1) * span)
        one = vectors[:, below, pl.ds(pl.multiple_of((1 - o) * block, block), block)].reshape(wide, block)
        two = vectors[:, below, 3 * block:].reshape(wide, block)
        summed = jnp.dot(kron, jnp.concatenate([one, two], axis=1), preferred_element_type=F32)
        for slot in range(2):
            partial[:, (3 + slot) * block + j * span:(3 + slot) * block + (j + 1) * span, :] = summed[
                :, slot * block:(slot + 1) * block
            ].reshape(local, span, block)

    to_next = [z - 1, z + 1]
    upstream = [last - z, z]
    downstream = [z, last - z]

    def chain_copy(side, c):
        return remote(
            leaving.at[side, c], arrived.at[side, c], chain_send.at[side, c], chain_recv.at[side, c],
            {"vec": to_next[side]},
        )

    def factor_copy(side):
        return remote(
            factor_out.at[side], factor_in.at[side], factor_send.at[side], factor_recv.at[side],
            {"vec": to_next[side]},
        )

    def cross_copy(side, c):
        return remote(
            leaving.at[side, c], crossed.at[c], chain_send.at[side, c], cross_recv.at[c],
            {"vec": to_next[side], "orb": 1 - o},
        )

    end_side = jnp.where(z == 0, 0, 1)

    def swap_copy(c):
        return remote(leaving.at[end_side, c], given.at[c], swap_send.at[c], swap_recv.at[c], {"orb": 1 - o})

    def part_of(side, c):
        return partial[side * half + c // PIECES, pl.ds(pl.multiple_of((c % PIECES) * piece, piece), piece), :]

    def give(c, carry):
        @pl.when(((z == 0) | (z == last)) & ((c // PIECES) % 2 != o))
        def _():
            leaving[end_side, c] = part_of(end_side, c).astype(BF16)
            swap_copy(c).start()

        return carry

    lax.fori_loop(0, chunks, give, jnp.int32(0))

    def chain_step(t, carry):
        for side in range(2):
            c = t - SKEW * upstream[side]
            head = upstream[side] == 0
            owner = downstream[side] == 0

            @pl.when((c >= 0) & (c < chunks))
            def _():
                own = part_of(side, c)
                here = (c // PIECES) % 2 == o

                @pl.when(head)
                def _():
                    leaving[side, c] = own.astype(BF16)

                @pl.when(jnp.logical_not(head) & jnp.logical_not(owner))
                def _():
                    chain_copy(side, c).wait_recv()
                    leaving[side, c] = (own + arrived[side, c].astype(F32)).astype(BF16)

                @pl.when(owner & here)
                def _():
                    chain_copy(side, c).wait_recv()
                    operator[o, c] = (own + arrived[side, c].astype(F32)).astype(BF16)
                    swap_copy(c).wait_recv()
                    cross_copy(side, c).wait_recv()
                    operator[1 - o, c] = (given[c].astype(F32) + crossed[c].astype(F32)).astype(BF16)

                @pl.when(jnp.logical_not(owner) & ((downstream[side] > 1) | here))
                def _():
                    chain_copy(side, c).start()

                @pl.when((downstream[side] == 1) & jnp.logical_not(here))
                def _():
                    cross_copy(side, c).start()

                @pl.when(c == 0)
                def _():
                    @pl.when(head)
                    def _():
                        factor_in[side] = jnp.zeros_like(factor)

                    @pl.when(jnp.logical_not(head))
                    def _():
                        factor_copy(side).wait_recv()

                    @pl.when(jnp.logical_not(owner))
                    def _():
                        factor_out[side] = factor_in[side] + factor
                        factor_copy(side).start()

        return carry

    at_end = (z == 0) | (z == last)
    base = jnp.where(z == 0, 0, half)
    inward = jnp.where(z == 0, 1, last - 1)
    rows_copy.wait_recv()

    share = rows // PARTS

    def place(w, part):
        return every.at[x * local + w, pl.ds(part * share, share)]

    def own_copies(i):
        w = base + 2 * i + o
        copies = []
        for core in range(2):
            copies.append((core, {"vec": inward, "orb": core}))
        for hop in range(1, width):
            for core in range(2):
                copies.append((core, {"walk": lax.rem(x + hop, width), "orb": core}))
        copies.append((1 - o, {"orb": 1 - o}))
        return [
            remote(
                result.at[i, core, pl.ds(part * share, share)], place(w, part),
                own_sends.at[i, n, part], every_recv.at[x, w, part], where,
            )
            for part in range(PARTS)
            for n, (core, where) in enumerate(copies)
        ]

    def finish(i):
        @pl.when(at_end)
        def _():
            a = 2 * i + o
            w = base + a

            def tile(core, slot):
                flat = operator[core, pl.ds(a * PIECES, PIECES)].reshape(packed, block)
                return flat[slot * block:(slot + 1) * block, :]

            def put(r, c, value):
                full[r * block:(r + 1) * block, c * block:(c + 1) * block] = value

            spots = (((0, 0), (0, 1), (0, 2), (1, 1), (1, 3)), ((2, 1), (2, 2), (2, 3), (3, 0), (3, 3)))
            for core in range(2):
                for slot in range(5):
                    r, c = spots[core][slot]
                    value = tile(core, slot)
                    put(r, c, value)
                    if r != c:
                        put(c, r, value.T)
            term[pl.ds(pl.multiple_of(o * rows, rows), rows), :] = walkers[w]
            term[pl.ds(pl.multiple_of((1 - o) * rows, rows), rows), :] = other_rows[w]
            running = term[...].astype(F32)
            for degree in range(1, ORDER + 1):
                fresh = (jnp.dot(full[...], term[...], preferred_element_type=F32) * (1.0 / degree)).astype(BF16)
                running = running + fresh.astype(F32)
                if degree < ORDER:
                    term[...] = fresh
            result[i] = running.astype(BF16).reshape(2, rows, electrons)
            for copy in own_copies(i):
                copy.start()
            every[x * local + w] = result[i, o]

    begun = 0
    for i in range(mine):
        until = SKEW * last + (2 * i + 2) * PIECES
        lax.fori_loop(begun, until, chain_step, jnp.int32(0))
        begun = until
        finish(i)


    def log_copy(hop):
        other = lax.rem(x + hop, width)
        return remote(logs.at[x], logs.at[x], log_send.at[hop - 1], log_recv.at[x], {"walk": other})

    walker_id = lax.broadcasted_iota(jnp.int32, factor.shape, 0)
    weights = jnp.zeros(factor.shape, F32)
    for w in range(local):
        weights = jnp.where(walker_id == w, log_weight[w], weights)
    logs[x] = weights + factor + factor_in[0] + factor_in[1]
    for hop in range(1, width):
        log_copy(hop).start()

    def onward(w, part, hop_to):
        spot = place(w, part)
        return remote(spot, spot, next_send.at[w, part], every_recv.at[x, w, part], {"vec": hop_to})

    def across(w, part, hop):
        spot = place(w, part)
        return remote(
            spot, spot, across_send.at[hop - 1, w, part], every_recv.at[x, w, part], {"walk": lax.rem(x + hop, width)}
        )

    near = jnp.where(z <= last - z, 0, 1)

    def route(side, a):
        w = side * half + a
        away = jnp.where(side == 0, z, last - z)
        hop_to = jnp.where(side == 0, z + 1, z - 1)
        return w, away, last - away, hop_to

    for i in range(mine):
        for side in (near, 1 - near):
            for part, a in [(part, a) for part in range(PARTS) for a in (2 * i, 2 * i + 1)]:
                w, away, end, hop_to = route(side, a)

                @pl.when(away > 0)
                def _():
                    onward(w, part, hop_to).wait_recv()

                    @pl.when(end > 0)
                    def _():
                        onward(w, part, hop_to).start()

                    for hop in range(1, width):
                        across(w, part, hop).start()

                @pl.when((away == 0) & (o != a % 2))
                def _():
                    onward(w, part, hop_to).wait_recv()

    for hop in range(1, width):
        other = lax.rem(x + hop, width)
        for w in range(local):
            for part in range(PARTS):
                spot = every.at[other * local + w, pl.ds(part * share, share)]
                remote(
                    spot, spot, across_send.at[hop - 1, w, part], every_recv.at[other, w, part], {"walk": other}
                ).wait_recv()
        remote(logs.at[other], logs.at[other], log_send.at[hop - 1], log_recv.at[other], {"walk": other}).wait_recv()

    for s in range(local):
        source = copy_list[s]
        out[s] = every[source]
        out_log[s] = jnp.max(logs[source // local, pl.ds(source % local, 1), :])

    rows_copy.wait_send()
    for hop in range(1, width):
        log_copy(hop).wait_send()

    def drain(c, carry):
        for side in range(2):
            @pl.when(downstream[side] > 0)
            def _():
                chain_copy(side, c).wait_send()

        @pl.when(at_end & ((c // PIECES) % 2 != o))
        def _():
            swap_copy(c).wait_send()

        return carry

    lax.fori_loop(0, chunks, drain, jnp.int32(0))
    for side in range(2):
        @pl.when(downstream[side] > 0)
        def _():
            factor_copy(side).wait_send()

    @pl.when(at_end)
    def _():
        for i in range(mine):
            for copy in own_copies(i):
                copy.wait_send()

    for a in range(half):
        for side in range(2):
            w = side * half + a
            _, away, end, hop_to = route(side, a)

            @pl.when(away > 0)
            def _():
                @pl.when(end > 0)
                def _():
                    for part in range(PARTS):
                        onward(w, part, hop_to).wait_send()

                for hop in range(1, width):
                    for part in range(PARTS):
                        across(w, part, hop).wait_send()


def per_device(depth, width, walkers, inv_intersection, trial, vectors, aux_field, log_weight, copy_list):
    local, rows, electrons = walkers.shape
    count, _, orbitals = vectors.shape
    half = local // 2
    block = orbitals // 4
    span = 2 * block // count
    wide = count * span
    packed = 5 * block
    piece = packed // PIECES
    chunks = half * PIECES
    mine = half // 2
    lanes = 128
    vmem = pl.BlockSpec(memory_space=pltpu.VMEM)
    smem = pl.BlockSpec(memory_space=pltpu.SMEM)
    dma = pltpu.SemaphoreType.DMA
    out, out_log = pl.pallas_call(
        functools.partial(kernel, depth, width),
        out_shape=(
            jax.ShapeDtypeStruct(walkers.shape, BF16),
            jax.ShapeDtypeStruct((local,), F32),
        ),
        in_specs=[vmem] * 5 + [smem] * 2,
        out_specs=(vmem, smem),
        scratch_shapes=[
            pltpu.VMEM((local, rows, electrons), BF16),
            pltpu.VMEM((count, rows, electrons), BF16),
            pltpu.VMEM((local, wide), F32),
            pltpu.VMEM((local, wide), F32),
            pltpu.VMEM((local, rows, electrons), BF16),
            pltpu.VMEM((local, packed, block), F32),
            pltpu.VMEM((2, chunks, piece, block), BF16),
            pltpu.VMEM((2, chunks, piece, block), BF16),
            pltpu.VMEM((chunks, piece, block), BF16),
            pltpu.VMEM((chunks, piece, block), BF16),
            pltpu.VMEM((2, chunks, piece, block), BF16),
            pltpu.VMEM((orbitals, orbitals), BF16),
            pltpu.VMEM((orbitals, electrons), BF16),
            pltpu.VMEM((mine, 2, rows, electrons), BF16),
            pltpu.VMEM((width * local, rows, electrons), BF16),
            pltpu.VMEM((2, local, lanes), F32),
            pltpu.VMEM((2, local, lanes), F32),
            pltpu.VMEM((width, local, lanes), F32),
            dma((2,)),
            dma((2,)),
            dma((2, chunks)),
            dma((2, chunks)),
            dma((2,)),
            dma((2,)),
            dma((chunks,)),
            dma((chunks,)),
            dma((chunks,)),
            dma((width, local, PARTS)),
            dma((mine, 2 * width + 1, PARTS)),
            dma((local, PARTS)),
            dma((max(width - 1, 1), local, PARTS)),
            dma((max(width - 1, 1),)),
            dma((width,)),
        ],
        compiler_params=pltpu.CompilerParams(collective_id=0, has_side_effects=True),
    )(walkers, inv_intersection, trial, vectors, aux_field, log_weight, copy_list)
    return out, out_log


def solution(mesh):
    depth, width = mesh.shape["vec"], mesh.shape["walk"]
    assert mesh.shape["orb"] == 2 and depth > 1
    return jax.shard_map(
        functools.partial(per_device, depth, width),
        mesh=mesh,
        in_specs=(
            P(("grp", "walk"), "orb", None),
            P(("grp", "walk"), None, None),
            P(),
            P("vec", "orb", None),
            P(("grp", "walk"), "vec"),
            P(("grp", "walk")),
            P(("grp", "walk")),
        ),
        out_specs=(P(("grp", "walk"), "orb", None), P(("grp", "walk"))),
        check_vma=False,
    )
```

profile of v0, /device:TPU:0, one launch (start us, length us, event | category | flops | bytes accessed | tf_op | source)
XLA Modules:
  0.0 54.4 jit_solution(928698976170805445)
XLA Ops:
  0.6 50.7 %shard_map.86 = (bf16[8,256,128]{2,1,0:T(8,128)(2,1)}, f32[8]{0:T(128)}) custom-call(bf16[8,256,128]{2,1,0:T(8,128)(2,1)} %walkers.1, bf16[8,128,128]{2,1,0:T(8,128)(2,1)} %inverse.1, bf16[512,128]{1,0:T(8,128)(2,1)} %trial.1, bf16[8,256,512]{2,1,0:T(8,128)(2,1)} %vectors.1, f32[8,8]{1,0:T(8,128)} %aux.1, f32[8]{0:T(128)} %log_weight.1, s32[8]{0:T(128)} %copy_list.1), custom_call_target="tpu_custom_call" | custom-call | tf_op jit(solution)/shard_map/pallas_call | solution.py:417
  51.4 1.9 %copy.11 = bf16[8,256,128]{2,1,0:T(8,128)(2,1)} copy(bf16[8,256,128]{2,1,0:T(8,128)(2,1)} %get-tuple-element.4) | data formatting | bytes 1048576
  53.3 1.1 %copy.12 = f32[8]{0:T(128)} copy(f32[8]{0:T(128)} %get-tuple-element.5) | data formatting | bytes 64
where the time goes:
time: 54.6 us; the launch traced here: 54.4 us
  Pallas kernels  50.7 us (93%)
  local copies, waits for them, and re-layouts  2.98 us (5%)
  between operations  0.64 us (1%)
    pallas_call x1, Pallas kernels, per_device(): pl.pallas_call(functools.partial(kernel, depth, width), out_shape=(jax.Sh...  50.7 us
    unnamed x2, local copies, waits for them, and re-layouts  2.98 us

commit v1 on v0

v1 whole, which is shorter than its diff:
```python
import functools
import math

import jax
import jax.numpy as jnp
from jax import lax
from jax.experimental import pallas as pl
from jax.experimental.pallas import tpu as pltpu
from jax.sharding import PartitionSpec as P

ORDER = 6
BLOCKS = 4
SKEW = 5
PARTS = 2
REACH = 3
MESH = pl.DeviceIdType.MESH
F32 = jnp.float32
BF16 = jnp.bfloat16

step_root = math.sqrt(0.08)


def remote(src, dst, send, recv, where):
    return pltpu.make_async_remote_copy(
        src_ref=src, dst_ref=dst, send_sem=send, recv_sem=recv, device_id=where, device_id_type=MESH
    )


def kernel(
    depth, width,
    walkers_in, inverse_in, trial_in, vectors_in, aux_in, log_in, copies_in,
    out, out_log,
    walkers, inverse, trial, vectors, aux, log_weight, copies,
    green, mixed, strips, level, bias_all, facts, picked, partial, leaving, arrived, given, crossed,
    extra_in, extra_out, edge, staged, pool, full, term, result, gathered,
    load_sems, copies_send, copies_recv, facts_send, facts_recv, bias_send, bias_recv,
    chain_send, chain_recv, cross_recv, swap_send, swap_recv, extra_send, extra_recv, edge_sems,
    stage_send, pool_recv, own_send, next_send, slot_recv, write_sems,
):
    z = lax.axis_index("vec")
    x = lax.axis_index("walk")
    o = lax.axis_index("orb")
    last = depth - 1
    local, rows, electrons = walkers.shape
    count, _, orbitals = vectors.shape
    half = local // 2
    block = orbitals // 4
    span = 2 * block // count
    wide = count * span
    chunks = half * BLOCKS
    mine = half // 2
    lanes = extra_in.shape[2]
    hops = range(1, width)

    barrier = pltpu.get_barrier_semaphore()

    def greet(where):
        pl.semaphore_signal(barrier, inc=1, device_id=where, device_id_type=MESH)

    greet({"orb": 1 - o})
    for hop in hops:
        for core in range(2):
            greet({"walk": lax.rem(x + hop, width), "orb": core})

    @pl.when(z > 0)
    def _():
        for core in range(2):
            greet({"vec": z - 1, "orb": core})

    @pl.when(z < last)
    def _():
        for core in range(2):
            greet({"vec": z + 1, "orb": core})

    pairs = (
        (copies_in, copies.at[x]), (log_in, log_weight), (walkers_in, walkers), (inverse_in, inverse), (trial_in, trial),
        (vectors_in, vectors), (aux_in, aux),
    )
    loads = [pltpu.make_async_copy(src, dst, load_sems.at[n]) for n, (src, dst) in enumerate(pairs)]
    for load in loads:
        load.start()

    loads[2].wait()
    loads[3].wait()
    for w in range(local):
        green[w] = jnp.dot(walkers[w], inverse[w], preferred_element_type=F32).astype(BF16)
    loads[4].wait()
    loads[5].wait()
    for g in range(count):
        mixed[g] = jnp.dot(vectors[g], trial[...], preferred_element_type=F32).astype(BF16)
    gram = jnp.zeros((local * span, wide), F32)
    for j in range(rows // span):
        left = green[:, j * span:(j + 1) * span, :].reshape(local * span, electrons)
        right = mixed[:, j * span:(j + 1) * span, :].reshape(wide, electrons)
        gram = gram + lax.dot_general(left, right, (((1,), (1,)), ((), ())), preferred_element_type=F32)
    row_id = lax.broadcasted_iota(jnp.int32, (local * span, wide), 0)
    col_id = lax.broadcasted_iota(jnp.int32, (local * span, wide), 1)
    same = row_id % span == col_id % span
    folded = jnp.sum(jnp.where(same, gram, 0.0).reshape(local, span, wide), axis=1)
    wide_row = lax.broadcasted_iota(jnp.int32, (wide, wide), 0)
    wide_col = lax.broadcasted_iota(jnp.int32, (wide, wide), 1)
    groups = jnp.where(wide_row // span == wide_col // span, 1.0, 0.0).astype(F32)
    bias_all[o, x] = jnp.dot(folded, groups, precision=lax.Precision.HIGHEST, preferred_element_type=F32)

    loads[6].wait()
    loads[0].wait()
    loads[1].wait()
    pick_row = lax.broadcasted_iota(jnp.int32, (count, wide), 0)
    pick_col = lax.broadcasted_iota(jnp.int32, (count, wide), 1)
    pick = jnp.where(pick_row == pick_col // span, 1.0, 0.0).astype(F32)
    facts[x, 0:local, :] = jnp.dot(aux[...], pick, precision=lax.Precision.HIGHEST, preferred_element_type=F32)
    walker_id = lax.broadcasted_iota(jnp.int32, (local, wide), 0)
    weights = jnp.zeros((local, wide), F32)
    for w in range(local):
        weights = jnp.where(walker_id == w, log_weight[w], weights)
    facts[x, local:2 * local, :] = weights

    sides = jnp.where(z > 0, 2, 0) + jnp.where(z < last, 2, 0)
    pl.semaphore_wait(barrier, 1 + 2 * (width - 1) + sides)

    bias_peers = [{"walk": lax.rem(x + hop, width), "orb": core} for hop in hops for core in range(2)] + [{"orb": 1 - o}]
    bias_copies = [
        remote(bias_all.at[o, x], bias_all.at[o, x], bias_send.at[n], bias_recv.at[o, x], where)
        for n, where in enumerate(bias_peers)
    ]
    for copy in bias_copies:
        copy.start()

    def facts_copy(hop, owner):
        return remote(
            facts.at[owner], facts.at[owner], facts_send.at[hop], facts_recv.at[owner], {"walk": lax.rem(x + hop, width)}
        )

    def copies_copy(hop, owner):
        return remote(
            copies.at[owner], copies.at[owner], copies_send.at[hop], copies_recv.at[owner],
            {"walk": lax.rem(x + hop, width)},
        )

    for hop in hops:
        copies_copy(hop, x).start()
        facts_copy(hop, x).start()

    chunk_row = lax.broadcasted_iota(jnp.int32, (count, span, block), 1)
    chunk_col = lax.broadcasted_iota(jnp.int32, (count, span, block), 2)
    crossing = jnp.zeros((count, span, block), F32)

    def columns(n):
        return pl.ds(pl.multiple_of(n * block, block), block)

    for j in range(block // span):
        here = slice(j * span, (j + 1) * span)
        below = slice(block + j * span, block + (j + 1) * span)
        first = vectors[:, here, columns(2 * o)].astype(F32)
        second = vectors[:, below, columns(1 + 2 * o)].astype(F32)
        crossing = crossing + jnp.where(chunk_row + j * span == chunk_col, second, 0.0)
        joined = jnp.where(chunk_row + j * span <= chunk_col, first, second).astype(BF16)
        strips[j, :, 0:block] = joined.reshape(wide, block)
        strips[j, :, block:2 * block] = vectors[:, here, block:2 * block].reshape(wide, block)
        strips[j, :, 2 * block:3 * block] = vectors[:, here, columns(2 + o)].reshape(wide, block)
        strips[j, :, 3 * block:] = vectors[:, below, columns(3 * (1 - o))].reshape(wide, block)
    level[...] = crossing.reshape(wide, block).astype(BF16)

    for hop in hops:
        other = lax.rem(x + hop, width)
        facts_copy(hop, other).wait_recv()
        for core in range(2):
            remote(
                bias_all.at[core, other], bias_all.at[core, other], bias_send.at[0], bias_recv.at[core, other], {"walk": other}
            ).wait_recv()
    remote(bias_all.at[1 - o, x], bias_all.at[1 - o, x], bias_send.at[0], bias_recv.at[1 - o, x], {"orb": 1 - o}).wait_recv()

    for s in range(local):
        source = copies[x, s]
        column = source // local
        at = source % local
        row = pl.ds(at, 1)
        picked[0, s:s + 1, :] = bias_all[0, column, row, :] + bias_all[1, column, row, :]
        picked[1, s:s + 1, :] = facts[column, row, :]
        picked[2, s:s + 1, :] = facts[column, pl.ds(local + at, 1), :]

    bias = picked[0]
    drawn = picked[1]
    shift = -step_root * bias
    field = drawn - shift
    factor = jnp.sum(drawn * shift - 0.5 * shift * shift, axis=1, keepdims=True) * (1.0 / span)
    factor = jnp.broadcast_to(factor, (local, lanes))
    weighted = (field * step_root).astype(BF16)
    spread = jnp.broadcast_to(weighted.astype(F32)[:, None, :], (local, span, wide)).reshape(local * span, wide)
    kron = jnp.where(same, spread, 0.0).astype(BF16)

    for j in range(block // span):
        summed = jnp.dot(kron, strips[j], preferred_element_type=F32)
        for n in range(BLOCKS):
            partial[:, n, j * span:(j + 1) * span, :] = summed[:, n * block:(n + 1) * block].reshape(local, span, block)
    edge_part = jnp.dot(weighted, level[...], preferred_element_type=F32)

    to_next = [z - 1, z + 1]
    upstream = [last - z, z]
    downstream = [z, last - z]
    at_end = (z == 0) | (z == last)
    end_side = jnp.where(z == 0, 0, 1)
    base = jnp.where(z == 0, 0, half)

    def chain_copy(side, c):
        return remote(
            leaving.at[side, c], arrived.at[side, c], chain_send.at[side, c], chain_recv.at[side, c],
            {"vec": to_next[side]},
        )

    def cross_copy(side, c):
        return remote(
            leaving.at[side, c], crossed.at[c], chain_send.at[side, c], cross_recv.at[c],
            {"vec": to_next[side], "orb": 1 - o},
        )

    def swap_copy(c):
        return remote(leaving.at[end_side, c], given.at[c], swap_send.at[c], swap_recv.at[c], {"orb": 1 - o})

    def extra_copy(side):
        return remote(
            extra_out.at[side], extra_in.at[side], extra_send.at[side], extra_recv.at[side], {"vec": to_next[side]}
        )

    def part_of(side, c):
        return partial[side * half + c // BLOCKS, c % BLOCKS]

    def chain_step(t, carry):
        for side in range(2):
            c = t - SKEW * upstream[side]
            head = upstream[side] == 0
            owner = downstream[side] == 0

            @pl.when((c >= 0) & (c < chunks) & jnp.logical_not(owner))
            def _():
                own = part_of(side, c)
                here = (c // BLOCKS) % 2 == o

                @pl.when(head)
                def _():
                    leaving[side, c] = own.astype(BF16)

                @pl.when(jnp.logical_not(head))
                def _():
                    chain_copy(side, c).wait_recv()
                    leaving[side, c] = (own + arrived[side, c].astype(F32)).astype(BF16)

                @pl.when((downstream[side] > 1) | here)
                def _():
                    chain_copy(side, c).start()

                @pl.when((downstream[side] == 1) & jnp.logical_not(here))
                def _():
                    cross_copy(side, c).start()

                @pl.when(c == 0)
                def _():
                    @pl.when(head)
                    def _():
                        extra_in[side] = jnp.zeros_like(extra_in[side])

                    @pl.when(jnp.logical_not(head))
                    def _():
                        extra_copy(side).wait_recv()

                    extra_out[side, 0:local, :] = extra_in[side, 0:local, :] + factor
                    extra_out[side, local:, :] = extra_in[side, local:, :] + edge_part
                    extra_copy(side).start()

        return carry

    lax.fori_loop(0, SKEW * (last - 1) + chunks, chain_step, jnp.int32(0))

    for hop in hops:
        copies_copy(hop, lax.rem(x + hop, width)).wait_recv()

    def stage_copy(hop, a):
        return remote(
            staged.at[hop, a], pool.at[x, a // 2, o], stage_send.at[hop, a], pool_recv.at[x, a // 2, o],
            {"walk": lax.rem(x + hop, width), "orb": a % 2},
        )

    def swap_core():
        return remote(edge.at[o], edge.at[o], edge_sems.at[0], edge_sems.at[1], {"orb": 1 - o})

    @pl.when(at_end)
    def _():
        for a in range(half):
            for hop in range(width):
                source = copies[lax.rem(x + hop, width), base + a]
                held = walkers[source % local]
                if hop > 0:
                    staged[hop, a] = held
                    stage_copy(hop, a).start()
                else:
                    @pl.when(a % 2 == o)
                    def _():
                        pool[x, a // 2, o] = held

                    @pl.when(a % 2 != o)
                    def _():
                        staged[hop, a] = held
                        stage_copy(hop, a).start()

        def give(c, carry):
            @pl.when((c // BLOCKS) % 2 != o)
            def _():
                leaving[end_side, c] = part_of(end_side, c).astype(BF16)
                swap_copy(c).start()

            return carry

        lax.fori_loop(0, chunks, give, jnp.int32(0))

        for side in range(2):
            @pl.when(end_side == side)
            def _():
                extra_copy(side).wait_recv()
        edge[o] = edge_part + extra_in[end_side, local:, :]
        swap_core().start()
        swap_core().wait_recv()

    share = rows // PARTS
    inward = jnp.where(z == 0, 1, last - 1)
    direct = [a == half - 1 and last <= REACH for a in range(half)]

    def place(w, part):
        return gathered.at[w, pl.ds(part * share, share)]

    def away_z(n):
        return jnp.where(z == 0, n, last - n)

    def spread_copies(a):
        w = base + a
        targets = []
        for n in (range(last, 0, -1) if direct[a] else (1,)):
            for core in (1 - a % 2, a % 2):
                targets.append((core, {"vec": away_z(n), "orb": core}))
        targets.append((1 - a % 2, {"orb": 1 - o}))
        return [
            remote(
                result.at[a // 2, core, pl.ds(part * share, share)], place(w, part),
                own_send.at[a // 2, n, part], slot_recv.at[w, part], where,
            )
            for n, (core, where) in enumerate(targets)
            for part in range(PARTS)
        ]

    def write_copy(w):
        return pltpu.make_async_copy(gathered.at[w], out.at[w], write_sems.at[w])

    upper = lax.broadcasted_iota(jnp.int32, (block, block), 0) < lax.broadcasted_iota(jnp.int32, (block, block), 1)
    level_mask = lax.broadcasted_iota(jnp.int32, (block, block), 0) == lax.broadcasted_iota(jnp.int32, (block, block), 1)

    def finish(a):
        w = base + a
        i = a // 2

        def put(r, c, value):
            full[columns(r), columns(c)] = value

        for n in range(BLOCKS):
            c = a * BLOCKS + n
            remote(
                leaving.at[end_side, c], arrived.at[end_side, c], chain_send.at[end_side, c], chain_recv.at[end_side, c],
                {"vec": inward},
            ).wait_recv()
            swap_copy(c).wait_recv()
            remote(
                leaving.at[end_side, c], crossed.at[c], chain_send.at[end_side, c], cross_recv.at[c],
                {"vec": inward, "orb": 1 - o},
            ).wait_recv()
            kept = part_of(end_side, c) + arrived[end_side, c].astype(F32)
            taken = given[c].astype(F32) + crossed[c].astype(F32)
            for core, value in ((o, kept), (1 - o, taken)):
                if n == 0:
                    flipped = value.T
                    line = edge[core, pl.ds(w, 1), :]
                    put(2 * core, 2 * core, jnp.where(upper | level_mask, value, flipped).astype(BF16))
                    low = jnp.where(level_mask, jnp.broadcast_to(line, (block, block)), jnp.where(upper, flipped, value))
                    put(2 * core + 1, 2 * core + 1, low.astype(BF16))
                else:
                    r, k = ((2 * core, 1), (2 * core, 2 + core), (2 * core + 1, 3 * (1 - core)))[n - 1]
                    value = value.astype(BF16)
                    put(r, k, value)
                    put(k, r, value.T)

        for hop in range(width):
            other = lax.rem(x + hop, width)
            for core in range(2):
                arrival = remote(
                    staged.at[0, 0], pool.at[other, i, core], stage_send.at[0, 0], pool_recv.at[other, i, core],
                    {"walk": other, "orb": core},
                )
                if hop > 0:
                    arrival.wait_recv()
                else:
                    @pl.when(core != o)
                    def _():
                        arrival.wait_recv()
        column = copies[x, w] // local
        for core in range(2):
            start = pool[0, i, core]
            for other in hops:
                start = jnp.where(column == other, pool[other, i, core], start)
            term[core * rows:(core + 1) * rows, :] = start
        running = term[...].astype(F32)
        for degree in range(1, ORDER + 1):
            fresh = (jnp.dot(full[...], term[...], preferred_element_type=F32) * (1.0 / degree)).astype(BF16)
            running = running + fresh.astype(F32)
            if degree < ORDER:
                term[...] = fresh
        result[i] = running.astype(BF16).reshape(2, rows, electrons)
        for copy in spread_copies(a):
            copy.start()
        gathered[w] = result[i, o]
        write_copy(w).start()

    for a in range(half):
        @pl.when(at_end & (a % 2 == o))
        def _():
            finish(a)

    new_log = picked[2][:, 0:lanes] + factor + extra_in[0, 0:local, :] + extra_in[1, 0:local, :]
    for s in range(local):
        out_log[s] = jnp.max(new_log[s:s + 1, :])

    def onward(w, part, hop_to):
        spot = place(w, part)
        return remote(spot, spot, next_send.at[w, part], slot_recv.at[w, part], {"vec": hop_to})

    near = jnp.where(z <= last - z, 0, 1)

    def route(side, a):
        w = side * half + a
        away = jnp.where(side == 0, z, last - z)
        hop_to = jnp.where(side == 0, z + 1, z - 1)
        return w, away, last - away, hop_to

    for a in range(half):
        for side in (near, 1 - near):
            w, away, end, hop_to = route(side, a)

            @pl.when((away > 0) | (o != a % 2))
            def _():
                for part in range(PARTS):
                    onward(w, part, hop_to).wait_recv()
                    if not direct[a]:
                        @pl.when((away > 0) & (end > 0))
                        def _():
                            onward(w, part, hop_to).start()
                write_copy(w).start()

    for w in range(local):
        write_copy(w).wait()

    for copy in bias_copies:
        copy.wait_send()
    for hop in hops:
        facts_copy(hop, x).wait_send()
        copies_copy(hop, x).wait_send()

    def drain(c, carry):
        for side in range(2):
            @pl.when(downstream[side] > 0)
            def _():
                chain_copy(side, c).wait_send()

        @pl.when(at_end & ((c // BLOCKS) % 2 != o))
        def _():
            swap_copy(c).wait_send()

        return carry

    lax.fori_loop(0, chunks, drain, jnp.int32(0))
    for side in range(2):
        @pl.when(downstream[side] > 0)
        def _():
            extra_copy(side).wait_send()

    @pl.when(at_end)
    def _():
        swap_core().wait_send()
        for a in range(half):
            for hop in range(width):
                if hop > 0:
                    stage_copy(hop, a).wait_send()
                else:
                    @pl.when(a % 2 != o)
                    def _():
                        stage_copy(hop, a).wait_send()

            @pl.when(a % 2 == o)
            def _():
                for copy in spread_copies(a):
                    copy.wait_send()

    for a in range(half):
        if not direct[a]:
            for side in range(2):
                w, away, end, hop_to = route(side, a)

                @pl.when((away > 0) & (end > 0))
                def _():
                    for part in range(PARTS):
                        onward(w, part, hop_to).wait_send()


def per_device(depth, width, walkers, inv_intersection, trial, vectors, aux_field, log_weight, copy_list):
    local, rows, electrons = walkers.shape
    count, _, orbitals = vectors.shape
    half = local // 2
    block = orbitals // 4
    span = 2 * block // count
    wide = count * span
    chunks = half * BLOCKS
    mine = half // 2
    lanes = 128
    reach = max(depth - 1, 1) if depth - 1 <= REACH else 1
    dma = pltpu.SemaphoreType.DMA
    anywhere = pl.BlockSpec(memory_space=pl.ANY)
    out, out_log = pl.pallas_call(
        functools.partial(kernel, depth, width),
        out_shape=(
            jax.ShapeDtypeStruct(walkers.shape, BF16),
            jax.ShapeDtypeStruct((local,), F32),
        ),
        in_specs=[anywhere] * 7,
        out_specs=(anywhere, pl.BlockSpec(memory_space=pltpu.SMEM)),
        scratch_shapes=[
            pltpu.VMEM(walkers.shape, BF16),
            pltpu.VMEM(inv_intersection.shape, BF16),
            pltpu.VMEM(trial.shape, BF16),
            pltpu.VMEM(vectors.shape, BF16),
            pltpu.VMEM(aux_field.shape, F32),
            pltpu.SMEM((local,), F32),
            pltpu.SMEM((width, local), jnp.int32),
            pltpu.VMEM((local, rows, electrons), BF16),
            pltpu.VMEM((count, rows, electrons), BF16),
            pltpu.VMEM((block // span, wide, BLOCKS * block), BF16),
            pltpu.VMEM((wide, block), BF16),
            pltpu.VMEM((2, width, local, wide), F32),
            pltpu.VMEM((width, 2 * local, wide), F32),
            pltpu.VMEM((3, local, wide), F32),
            pltpu.VMEM((local, BLOCKS, block, block), F32),
            pltpu.VMEM((2, chunks, block, block), BF16),
            pltpu.VMEM((2, chunks, block, block), BF16),
            pltpu.VMEM((chunks, block, block), BF16),
            pltpu.VMEM((chunks, block, block), BF16),
            pltpu.VMEM((2, 2 * local, lanes), F32),
            pltpu.VMEM((2, 2 * local, lanes), F32),
            pltpu.VMEM((2, local, lanes), F32),
            pltpu.VMEM((width, half, rows, electrons), BF16),
            pltpu.VMEM((width, mine, 2, rows, electrons), BF16),
            pltpu.VMEM((orbitals, orbitals), BF16),
            pltpu.VMEM((orbitals, electrons), BF16),
            pltpu.VMEM((mine, 2, rows, electrons), BF16),
            pltpu.VMEM((local, rows, electrons), BF16),
            dma((7,)),
            dma((width,)),
            dma((width,)),
            dma((width,)),
            dma((width,)),
            dma((2 * width,)),
            dma((2, width)),
            dma((2, chunks)),
            dma((2, chunks)),
            dma((chunks,)),
            dma((chunks,)),
            dma((chunks,)),
            dma((2,)),
            dma((2,)),
            dma((2,)),
            dma((width, half)),
            dma((width, mine, 2)),
            dma((mine, 2 * reach + 1, PARTS)),
            dma((local, PARTS)),
            dma((local, PARTS)),
            dma((local,)),
        ],
        compiler_params=pltpu.CompilerParams(collective_id=0, has_side_effects=True),
    )(walkers, inv_intersection, trial, vectors, aux_field, log_weight, copy_list)
    return out, out_log


def solution(mesh):
    depth, width = mesh.shape["vec"], mesh.shape["walk"]
    assert mesh.shape["orb"] == 2 and depth > 1
    return jax.shard_map(
        functools.partial(per_device, depth, width),
        mesh=mesh,
        in_specs=(
            P(("grp", "walk"), "orb", None),
            P(("grp", "walk"), None, None),
            P(),
            P("vec", "orb", None),
            P(("grp", "walk"), "vec"),
            P(("grp", "walk")),
            P(("grp", "walk")),
        ),
        out_specs=(P(("grp", "walk"), "orb", None), P(("grp", "walk"))),
        check_vma=False,
    )
```

time: 54.6 us -> 52.3 us (0.958)
  Pallas kernels: 50.7 us -> 48.5 us
    pallas_call x1, Pallas kernels: 50.7 us -> 48.5 us  [per_device(): pl.pallas_call(functools.partial(kernel, depth, width), out_shape=(jax.Sh...]
where the time goes in v1:
time: 52.3 us; the launch traced here: 52.1 us
  Pallas kernels  48.5 us (93%)
  local copies, waits for them, and re-layouts  2.98 us (6%)
  between operations  0.64 us (1%)
    pallas_call x1, Pallas kernels, per_device(): pl.pallas_call(functools.partial(kernel, depth, width), out_shape=(jax.Sh...  48.5 us
    unnamed x2, local copies, waits for them, and re-layouts  2.98 us

profile of v1, /device:TPU:0, one launch (start us, length us, event | category | flops | bytes accessed | tf_op | source)
XLA Modules:
  0.0 52.1 jit_solution(17423600888499172153)
XLA Ops:
  0.6 48.5 %shard_map.86 = (bf16[8,256,128]{2,1,0:T(8,128)(2,1)}, f32[8]{0:T(128)}) custom-call(bf16[8,256,128]{2,1,0:T(8,128)(2,1)} %walkers_in.1, bf16[8,128,128]{2,1,0:T(8,128)(2,1)} %inverse_in.1, bf16[512,128]{1,0:T(8,128)(2,1)} %trial_in.1, bf16[8,256,512]{2,1,0:T(8,128)(2,1)} %vectors_in.1, f32[8,8]{1,0:T(8,128)} %aux_in.1, f32[8]{0:T(128)} %log_in.1, s32[8]{0:T(128)} %copies_in.1), custom_call_target="tpu_custom_call" | custom-call | tf_op jit(solution)/shard_map/pallas_call | solution.py:522
  49.2 1.9 %copy.11 = bf16[8,256,128]{2,1,0:T(8,128)(2,1)} copy(bf16[8,256,128]{2,1,0:T(8,128)(2,1)} %get-tuple-element.4) | data formatting | bytes 1048576
  51.0 1.1 %copy.12 = f32[8]{0:T(128)} copy(f32[8]{0:T(128)} %get-tuple-element.5) | data formatting | bytes 64

commit v2 on v1

--- a/solution.py
+++ b/solution.py
@@ -322,7 +322,8 @@
 
     share = rows // PARTS
     inward = jnp.where(z == 0, 1, last - 1)
-    direct = [a == half - 1 and last <= REACH for a in range(half)]
+    short = last <= REACH
+    plans = [tuple(range(last if a == half - 1 else min(last, 2), 0, -1)) if short else (1,) for a in range(half)]
 
     def place(w, part):
         return gathered.at[w, pl.ds(part * share, share)]
@@ -333,7 +334,7 @@
     def spread_copies(a):
         w = base + a
         targets = []
-        for n in (range(last, 0, -1) if direct[a] else (1,)):
+        for n in plans[a]:
             for core in (1 - a % 2, a % 2):
                 targets.append((core, {"vec": away_z(n), "orb": core}))
         targets.append((1 - a % 2, {"orb": 1 - o}))
@@ -445,8 +446,8 @@
             def _():
                 for part in range(PARTS):
                     onward(w, part, hop_to).wait_recv()
-                    if not direct[a]:
-                        @pl.when((away > 0) & (end > 0))
+                    if plans[a][0] < last:
+                        @pl.when((away >= plans[a][0]) & (end > 0))
                         def _():
                             onward(w, part, hop_to).start()
                 write_copy(w).start()
@@ -496,11 +497,11 @@
                     copy.wait_send()
 
     for a in range(half):
-        if not direct[a]:
+        if plans[a][0] < last:
             for side in range(2):
                 w, away, end, hop_to = route(side, a)
 
-                @pl.when((away > 0) & (end > 0))
+                @pl.when((away >= plans[a][0]) & (end > 0))
                 def _():
                     for part in range(PARTS):
                         onward(w, part, hop_to).wait_send()

time: 52.3 us -> 49.1 us (0.939)
  Pallas kernels: 48.5 us -> 45.3 us
    pallas_call x1, Pallas kernels: 48.5 us -> 45.3 us  [per_device(): pl.pallas_call(functools.partial(kernel, depth, width), out_shape=(jax.Sh...]
where the time goes in v2:
time: 49.1 us; the launch traced here: 48.9 us
  Pallas kernels  45.3 us (92%)
  local copies, waits for them, and re-layouts  2.98 us (6%)
  between operations  0.64 us (1%)
    pallas_call x1, Pallas kernels, per_device(): pl.pallas_call(functools.partial(kernel, depth, width), out_shape=(jax.Sh...  45.3 us
    unnamed x2, local copies, waits for them, and re-layouts  2.98 us

profile of v2, /device:TPU:0, one launch (start us, length us, event | category | flops | bytes accessed | tf_op | source)
XLA Modules:
  0.0 48.9 jit_solution(670011051068543637)
XLA Ops:
  0.6 45.3 %shard_map.86 = (bf16[8,256,128]{2,1,0:T(8,128)(2,1)}, f32[8]{0:T(128)}) custom-call(bf16[8,256,128]{2,1,0:T(8,128)(2,1)} %walkers_in.1, bf16[8,128,128]{2,1,0:T(8,128)(2,1)} %inverse_in.1, bf16[512,128]{1,0:T(8,128)(2,1)} %trial_in.1, bf16[8,256,512]{2,1,0:T(8,128)(2,1)} %vectors_in.1, f32[8,8]{1,0:T(8,128)} %aux_in.1, f32[8]{0:T(128)} %log_in.1, s32[8]{0:T(128)} %copies_in.1), custom_call_target="tpu_custom_call" | custom-call | tf_op jit(solution)/shard_map/pallas_call | solution.py:523
  45.9 1.9 %copy.11 = bf16[8,256,128]{2,1,0:T(8,128)(2,1)} copy(bf16[8,256,128]{2,1,0:T(8,128)(2,1)} %get-tuple-element.4) | data formatting | bytes 1048576
  47.8 1.1 %copy.12 = f32[8]{0:T(128)} copy(f32[8]{0:T(128)} %get-tuple-element.5) | data formatting | bytes 64

commit v3 on v2

--- a/solution.py
+++ b/solution.py
@@ -10,9 +10,11 @@
 
 ORDER = 6
 BLOCKS = 4
-SKEW = 5
+SUB = 2
+SKEW = 10
 PARTS = 2
 REACH = 3
+PLANS = ((2, -1, 1), (3, 2, 1), (2, 1), (2, 1))
 MESH = pl.DeviceIdType.MESH
 F32 = jnp.float32
 BF16 = jnp.bfloat16
@@ -32,9 +34,9 @@
     out, out_log,
     walkers, inverse, trial, vectors, aux, log_weight, copies,
     green, mixed, strips, level, bias_all, facts, picked, partial, leaving, arrived, given, crossed,
-    extra_in, extra_out, edge, staged, pool, full, term, result, gathered,
+    back, extra_in, extra_out, edge, staged, pool, full, term, result, gathered,
     load_sems, copies_send, copies_recv, facts_send, facts_recv, bias_send, bias_recv,
-    chain_send, chain_recv, cross_recv, swap_send, swap_recv, extra_send, extra_recv, edge_sems,
+    chain_send, chain_recv, cross_recv, back_recv, swap_send, swap_recv, extra_send, extra_recv, edge_sems,
     stage_send, pool_recv, own_send, next_send, slot_recv, write_sems,
 ):
     z = lax.axis_index("vec")
@@ -47,9 +49,12 @@
     block = orbitals // 4
     span = 2 * block // count
     wide = count * span
-    chunks = half * BLOCKS
+    piece = block // SUB
+    each = BLOCKS * SUB
+    chunks = half * each
     mine = half // 2
     lanes = extra_in.shape[2]
+    insets = [1 if a == half - 1 and last >= REACH else 0 for a in range(half)]
     hops = range(1, width)
 
     barrier = pltpu.get_barrier_semaphore()
@@ -199,8 +204,13 @@
     upstream = [last - z, z]
     downstream = [z, last - z]
     at_end = (z == 0) | (z == last)
-    end_side = jnp.where(z == 0, 0, 1)
-    base = jnp.where(z == 0, 0, half)
+    near = jnp.where(z <= last - z, 0, 1)
+    base = near * half
+    inward = jnp.where(near == 0, z + 1, z - 1)
+    at_owner = [(z == n) | (z == last - n) for n in insets]
+
+    def depth_of(c):
+        return sum(jnp.where(c // each == a, n, 0) for a, n in enumerate(insets) if n) + jnp.int32(0)
 
     def chain_copy(side, c):
         return remote(
@@ -215,26 +225,33 @@
         )
 
     def swap_copy(c):
-        return remote(leaving.at[end_side, c], given.at[c], swap_send.at[c], swap_recv.at[c], {"orb": 1 - o})
+        return remote(leaving.at[near, c], given.at[c], swap_send.at[c], swap_recv.at[c], {"orb": 1 - o})
 
     def extra_copy(side):
         return remote(
             extra_out.at[side], extra_in.at[side], extra_send.at[side], extra_recv.at[side], {"vec": to_next[side]}
         )
 
+    def back_copy(c):
+        return remote(
+            leaving.at[near, c], back.at[o, c], chain_send.at[near, c], back_recv.at[o, c],
+            {"vec": inward, "orb": (c // each) % 2},
+        )
+
     def part_of(side, c):
-        return partial[side * half + c // BLOCKS, c % BLOCKS]
+        at = c % each
+        return partial[side * half + c // each, at // SUB, pl.ds(pl.multiple_of((at % SUB) * piece, piece), piece), :]
 
     def chain_step(t, carry):
         for side in range(2):
             c = t - SKEW * upstream[side]
             head = upstream[side] == 0
-            owner = downstream[side] == 0
-
-            @pl.when((c >= 0) & (c < chunks) & jnp.logical_not(owner))
+            togo = downstream[side] - depth_of(c)
+
+            @pl.when((c >= 0) & (c < chunks) & (togo > 0))
             def _():
                 own = part_of(side, c)
-                here = (c // BLOCKS) % 2 == o
+                here = (c // each) % 2 == o
 
                 @pl.when(head)
                 def _():
@@ -245,11 +262,11 @@
                     chain_copy(side, c).wait_recv()
                     leaving[side, c] = (own + arrived[side, c].astype(F32)).astype(BF16)
 
-                @pl.when((downstream[side] > 1) | here)
+                @pl.when((togo > 1) | here)
                 def _():
                     chain_copy(side, c).start()
 
-                @pl.when((downstream[side] == 1) & jnp.logical_not(here))
+                @pl.when((togo == 1) & jnp.logical_not(here))
                 def _():
                     cross_copy(side, c).start()
 
@@ -283,9 +300,9 @@
     def swap_core():
         return remote(edge.at[o], edge.at[o], edge_sems.at[0], edge_sems.at[1], {"orb": 1 - o})
 
-    @pl.when(at_end)
-    def _():
-        for a in range(half):
+    for a in range(half):
+        @pl.when(at_owner[a])
+        def _():
             for hop in range(width):
                 source = copies[lax.rem(x + hop, width), base + a]
                 held = walkers[source % local]
@@ -302,34 +319,56 @@
                         staged[hop, a] = held
                         stage_copy(hop, a).start()
 
-        def give(c, carry):
-            @pl.when((c // BLOCKS) % 2 != o)
-            def _():
-                leaving[end_side, c] = part_of(end_side, c).astype(BF16)
-                swap_copy(c).start()
-
-            return carry
-
-        lax.fori_loop(0, chunks, give, jnp.int32(0))
-
-        for side in range(2):
-            @pl.when(end_side == side)
-            def _():
-                extra_copy(side).wait_recv()
-        edge[o] = edge_part + extra_in[end_side, local:, :]
+            @pl.when(a % 2 != o)
+            def _():
+                def give(c, carry):
+                    leaving[near, c] = part_of(near, c).astype(BF16)
+                    swap_copy(c).start()
+                    return carry
+
+                lax.fori_loop(a * each, (a + 1) * each, give, jnp.int32(0))
+
+        if insets[a]:
+            @pl.when(at_end)
+            def _():
+                def back_step(c, carry):
+                    leaving[near, c] = part_of(near, c).astype(BF16)
+                    back_copy(c).start()
+                    return carry
+
+                lax.fori_loop(a * each, (a + 1) * each, back_step, jnp.int32(0))
+
+    for side in range(2):
+        @pl.when(at_end & (near == side))
+        def _():
+            extra_copy(side).wait_recv()
+
+    owning = functools.reduce(jnp.logical_or, at_owner)
+
+    @pl.when(owning)
+    def _():
+        edge[o] = edge_part + extra_in[0, local:, :] + extra_in[1, local:, :]
         swap_core().start()
         swap_core().wait_recv()
 
     share = rows // PARTS
-    inward = jnp.where(z == 0, 1, last - 1)
     short = last <= REACH
-    plans = [tuple(range(last if a == half - 1 else min(last, 2), 0, -1)) if short else (1,) for a in range(half)]
+    plans = [
+        tuple(n for n in PLANS[min(half - a, len(PLANS)) - 1] if -insets[a] <= n <= last - insets[a])
+        if short else (1,) + (-1,) * insets[a] for a in range(half)
+    ]
+
+    def passes(a, away):
+        if not short:
+            return (away > 0) & (away < last - insets[a])
+        gaps = [away == n for n in range(1, last - insets[a]) if n + 1 not in plans[a]]
+        return functools.reduce(jnp.logical_or, gaps, jnp.bool_(False))
 
     def place(w, part):
         return gathered.at[w, pl.ds(part * share, share)]
 
     def away_z(n):
-        return jnp.where(z == 0, n, last - n)
+        return jnp.where(near == 0, z + n, z - n)
 
     def spread_copies(a):
         w = base + a
@@ -361,18 +400,28 @@
             full[columns(r), columns(c)] = value
 
         for n in range(BLOCKS):
-            c = a * BLOCKS + n
-            remote(
-                leaving.at[end_side, c], arrived.at[end_side, c], chain_send.at[end_side, c], chain_recv.at[end_side, c],
-                {"vec": inward},
-            ).wait_recv()
-            swap_copy(c).wait_recv()
-            remote(
-                leaving.at[end_side, c], crossed.at[c], chain_send.at[end_side, c], cross_recv.at[c],
-                {"vec": inward, "orb": 1 - o},
-            ).wait_recv()
-            kept = part_of(end_side, c) + arrived[end_side, c].astype(F32)
-            taken = given[c].astype(F32) + crossed[c].astype(F32)
+            first_c = a * each + n * SUB
+            for c in range(first_c, first_c + SUB):
+                remote(
+                    leaving.at[near, c], arrived.at[near, c], chain_send.at[near, c], chain_recv.at[near, c], {"vec": inward}
+                ).wait_recv()
+                swap_copy(c).wait_recv()
+                remote(
+                    leaving.at[near, c], crossed.at[c], chain_send.at[near, c], cross_recv.at[c],
+                    {"vec": inward, "orb": 1 - o},
+                ).wait_recv()
+                if insets[a]:
+                    for core in range(2):
+                        remote(
+                            leaving.at[near, c], back.at[core, c], chain_send.at[near, c], back_recv.at[core, c],
+                            {"vec": away_z(-1), "orb": core},
+                        ).wait_recv()
+            run = pl.ds(first_c, SUB)
+            kept = partial[w, n] + arrived[near, run].reshape(block, block).astype(F32)
+            taken = given[run].reshape(block, block).astype(F32) + crossed[run].reshape(block, block).astype(F32)
+            if insets[a]:
+                kept = kept + back[o, run].reshape(block, block).astype(F32)
+                taken = taken + back[1 - o, run].reshape(block, block).astype(F32)
             for core, value in ((o, kept), (1 - o, taken)):
                 if n == 0:
                     flipped = value.T
@@ -418,7 +467,7 @@
         write_copy(w).start()
 
     for a in range(half):
-        @pl.when(at_end & (a % 2 == o))
+        @pl.when(at_owner[a] & (a % 2 == o))
         def _():
             finish(a)
 
@@ -430,26 +479,24 @@
         spot = place(w, part)
         return remote(spot, spot, next_send.at[w, part], slot_recv.at[w, part], {"vec": hop_to})
 
-    near = jnp.where(z <= last - z, 0, 1)
-
     def route(side, a):
         w = side * half + a
-        away = jnp.where(side == 0, z, last - z)
+        away = jnp.where(side == 0, z, last - z) - insets[a]
         hop_to = jnp.where(side == 0, z + 1, z - 1)
-        return w, away, last - away, hop_to
+        return w, away, hop_to
 
     for a in range(half):
         for side in (near, 1 - near):
-            w, away, end, hop_to = route(side, a)
-
-            @pl.when((away > 0) | (o != a % 2))
+            w, away, hop_to = route(side, a)
+
+            @pl.when((away != 0) | (o != a % 2))
             def _():
                 for part in range(PARTS):
                     onward(w, part, hop_to).wait_recv()
-                    if plans[a][0] < last:
-                        @pl.when((away >= plans[a][0]) & (end > 0))
-                        def _():
-                            onward(w, part, hop_to).start()
+
+                    @pl.when(passes(a, away))
+                    def _():
+                        onward(w, part, hop_to).start()
                 write_copy(w).start()
 
     for w in range(local):
@@ -463,13 +510,9 @@
 
     def drain(c, carry):
         for side in range(2):
-            @pl.when(downstream[side] > 0)
+            @pl.when(downstream[side] - depth_of(c) > 0)
             def _():
                 chain_copy(side, c).wait_send()
-
-        @pl.when(at_end & ((c // BLOCKS) % 2 != o))
-        def _():
-            swap_copy(c).wait_send()
 
         return carry
 
@@ -479,32 +522,48 @@
         def _():
             extra_copy(side).wait_send()
 
-    @pl.when(at_end)
+    @pl.when(owning)
     def _():
         swap_core().wait_send()
-        for a in range(half):
-            for hop in range(width):
-                if hop > 0:
-                    stage_copy(hop, a).wait_send()
-                else:
-                    @pl.when(a % 2 != o)
-                    def _():
-                        stage_copy(hop, a).wait_send()
+
+    for a in range(half):
+        @pl.when(at_owner[a])
+        def _():
+            for hop in hops:
+                stage_copy(hop, a).wait_send()
+
+            @pl.when(a % 2 != o)
+            def _():
+                stage_copy(0, a).wait_send()
+
+                def taken_back(c, carry):
+                    swap_copy(c).wait_send()
+                    return carry
+
+                lax.fori_loop(a * each, (a + 1) * each, taken_back, jnp.int32(0))
 
             @pl.when(a % 2 == o)
             def _():
                 for copy in spread_copies(a):
                     copy.wait_send()
 
+        if insets[a]:
+            @pl.when(at_end)
+            def _():
+                def back_done(c, carry):
+                    back_copy(c).wait_send()
+                    return carry
+
+                lax.fori_loop(a * each, (a + 1) * each, back_done, jnp.int32(0))
+
     for a in range(half):
-        if plans[a][0] < last:
-            for side in range(2):
-                w, away, end, hop_to = route(side, a)
-
-                @pl.when((away >= plans[a][0]) & (end > 0))
-                def _():
-                    for part in range(PARTS):
-                        onward(w, part, hop_to).wait_send()
+        for side in range(2):
+            w, away, hop_to = route(side, a)
+
+            @pl.when(passes(a, away))
+            def _():
+                for part in range(PARTS):
+                    onward(w, part, hop_to).wait_send()
 
 
 def per_device(depth, width, walkers, inv_intersection, trial, vectors, aux_field, log_weight, copy_list):
@@ -514,10 +573,11 @@
     block = orbitals // 4
     span = 2 * block // count
     wide = count * span
-    chunks = half * BLOCKS
+    piece = block // SUB
+    chunks = half * BLOCKS * SUB
     mine = half // 2
     lanes = 128
-    reach = max(depth - 1, 1) if depth - 1 <= REACH else 1
+    reach = max(max(depth - 1, 1) if depth - 1 <= REACH else 1, 2)
     dma = pltpu.SemaphoreType.DMA
     anywhere = pl.BlockSpec(memory_space=pl.ANY)
     out, out_log = pl.pallas_call(
@@ -544,10 +604,11 @@
             pltpu.VMEM((width, 2 * local, wide), F32),
             pltpu.VMEM((3, local, wide), F32),
             pltpu.VMEM((local, BLOCKS, block, block), F32),
-            pltpu.VMEM((2, chunks, block, block), BF16),
-            pltpu.VMEM((2, chunks, block, block), BF16),
-            pltpu.VMEM((chunks, block, block), BF16),
-            pltpu.VMEM((chunks, block, block), BF16),
+            pltpu.VMEM((2, chunks, piece, block), BF16),
+            pltpu.VMEM((2, chunks, piece, block), BF16),
+            pltpu.VMEM((chunks, piece, block), BF16),
+            pltpu.VMEM((chunks, piece, block), BF16),
+            pltpu.VMEM((2, chunks, piece, block), BF16),
             pltpu.VMEM((2, 2 * local, lanes), F32),
             pltpu.VMEM((2, 2 * local, lanes), F32),
             pltpu.VMEM((2, local, lanes), F32),
@@ -567,6 +628,7 @@
             dma((2, chunks)),
             dma((2, chunks)),
             dma((chunks,)),
+            dma((2, chunks)),
             dma((chunks,)),
             dma((chunks,)),
             dma((2,)),

time: 49.1 us -> 48.5 us (0.988)
  Pallas kernels: 45.3 us -> 44.6 us
    pallas_call x1, Pallas kernels: 45.3 us -> 44.6 us  [per_device(): pl.pallas_call(functools.partial(kernel, depth, width), out_shape=(jax.Sh...]
where the time goes in v3:
time: 48.5 us; the launch traced here: 48.3 us
  Pallas kernels  44.6 us (92%)
  local copies, waits for them, and re-layouts  2.98 us (6%)
  between operations  0.64 us (1%)
    pallas_call x1, Pallas kernels, per_device(): pl.pallas_call(functools.partial(kernel, depth, width), out_shape=(jax.Sh...  44.6 us
    unnamed x2, local copies, waits for them, and re-layouts  2.98 us

profile of v3, /device:TPU:0, one launch (start us, length us, event | category | flops | bytes accessed | tf_op | source)
XLA Modules:
  0.0 48.3 jit_solution(17219330975995398506)
XLA Ops:
  0.6 44.6 %shard_map.86 = (bf16[8,256,128]{2,1,0:T(8,128)(2,1)}, f32[8]{0:T(128)}) custom-call(bf16[8,256,128]{2,1,0:T(8,128)(2,1)} %walkers_in.1, bf16[8,128,128]{2,1,0:T(8,128)(2,1)} %inverse_in.1, bf16[512,128]{1,0:T(8,128)(2,1)} %trial_in.1, bf16[8,256,512]{2,1,0:T(8,128)(2,1)} %vectors_in.1, f32[8,8]{1,0:T(8,128)} %aux_in.1, f32[8]{0:T(128)} %log_in.1, s32[8]{0:T(128)} %copies_in.1), custom_call_target="tpu_custom_call" | custom-call | tf_op jit(solution)/shard_map/pallas_call | solution.py:583
  45.3 1.9 %copy.11 = bf16[8,256,128]{2,1,0:T(8,128)(2,1)} copy(bf16[8,256,128]{2,1,0:T(8,128)(2,1)} %get-tuple-element.4) | data formatting | bytes 1048576
  47.2 1.1 %copy.12 = f32[8]{0:T(128)} copy(f32[8]{0:T(128)} %get-tuple-element.5) | data formatting | bytes 64

commit v4 on v3

--- a/solution.py
+++ b/solution.py
@@ -10,8 +10,8 @@
 
 ORDER = 6
 BLOCKS = 4
-SUB = 2
-SKEW = 10
+SUB = 1
+SKEW = 5
 PARTS = 2
 REACH = 3
 PLANS = ((2, -1, 1), (3, 2, 1), (2, 1), (2, 1))
@@ -34,11 +34,12 @@
     out, out_log,
     walkers, inverse, trial, vectors, aux, log_weight, copies,
     green, mixed, strips, level, bias_all, facts, picked, partial, leaving, arrived, given, crossed,
-    back, extra_in, extra_out, edge, staged, pool, full, term, result, gathered,
+    back, extra_in, extra_out, edge, staged, pool, full, term, result,
     load_sems, copies_send, copies_recv, facts_send, facts_recv, bias_send, bias_recv,
     chain_send, chain_recv, cross_recv, back_recv, swap_send, swap_recv, extra_send, extra_recv, edge_sems,
-    stage_send, pool_recv, own_send, next_send, slot_recv, write_sems,
+    stage_send, pool_recv, own_send, next_send, slot_recv,
 ):
+    gathered = out
     z = lax.axis_index("vec")
     x = lax.axis_index("walk")
     o = lax.axis_index("orb")
@@ -385,9 +386,6 @@
             for n, (core, where) in enumerate(targets)
             for part in range(PARTS)
         ]
-
-    def write_copy(w):
-        return pltpu.make_async_copy(gathered.at[w], out.at[w], write_sems.at[w])
 
     upper = lax.broadcasted_iota(jnp.int32, (block, block), 0) < lax.broadcasted_iota(jnp.int32, (block, block), 1)
     level_mask = lax.broadcasted_iota(jnp.int32, (block, block), 0) == lax.broadcasted_iota(jnp.int32, (block, block), 1)
@@ -464,7 +462,6 @@
         for copy in spread_copies(a):
             copy.start()
         gathered[w] = result[i, o]
-        write_copy(w).start()
 
     for a in range(half):
         @pl.when(at_owner[a] & (a % 2 == o))
@@ -472,8 +469,7 @@
             finish(a)
 
     new_log = picked[2][:, 0:lanes] + factor + extra_in[0, 0:local, :] + extra_in[1, 0:local, :]
-    for s in range(local):
-        out_log[s] = jnp.max(new_log[s:s + 1, :])
+    out_log[...] = new_log
 
     def onward(w, part, hop_to):
         spot = place(w, part)
@@ -497,10 +493,7 @@
                     @pl.when(passes(a, away))
                     def _():
                         onward(w, part, hop_to).start()
-                write_copy(w).start()
-
-    for w in range(local):
-        write_copy(w).wait()
+
 
     for copy in bias_copies:
         copy.wait_send()
@@ -583,11 +576,11 @@
     out, out_log = pl.pallas_call(
         functools.partial(kernel, depth, width),
         out_shape=(
-            jax.ShapeDtypeStruct(walkers.shape, BF16),
-            jax.ShapeDtypeStruct((local,), F32),
+            pltpu.VMEM(walkers.shape, BF16),
+            pltpu.VMEM((local, 128), F32),
         ),
         in_specs=[anywhere] * 7,
-        out_specs=(anywhere, pl.BlockSpec(memory_space=pltpu.SMEM)),
+        out_specs=(pl.BlockSpec(memory_space=pltpu.VMEM), pl.BlockSpec(memory_space=pltpu.VMEM)),
         scratch_shapes=[
             pltpu.VMEM(walkers.shape, BF16),
             pltpu.VMEM(inv_intersection.shape, BF16),
@@ -617,7 +610,6 @@
             pltpu.VMEM((orbitals, orbitals), BF16),
             pltpu.VMEM((orbitals, electrons), BF16),
             pltpu.VMEM((mine, 2, rows, electrons), BF16),
-            pltpu.VMEM((local, rows, electrons), BF16),
             dma((7,)),
             dma((width,)),
             dma((width,)),
@@ -639,11 +631,27 @@
             dma((mine, 2 * reach + 1, PARTS)),
             dma((local, PARTS)),
             dma((local, PARTS)),
-            dma((local,)),
         ],
         compiler_params=pltpu.CompilerParams(collective_id=0, has_side_effects=True),
     )(walkers, inv_intersection, trial, vectors, aux_field, log_weight, copy_list)
-    return out, out_log
+
+    def settle(out_ref, log_ref, o1, o2, flat, sems):
+        c1 = pltpu.make_async_copy(out_ref, o1, sems.at[0])
+        c1.start()
+        for s in range(local):
+            flat[s] = jnp.max(log_ref[s:s + 1, :])
+        c2 = pltpu.make_async_copy(flat, o2, sems.at[1])
+        c2.start()
+        c1.wait()
+        c2.wait()
+
+    return pl.pallas_call(
+        settle,
+        out_shape=(jax.ShapeDtypeStruct(walkers.shape, BF16), jax.ShapeDtypeStruct((local,), F32)),
+        in_specs=[pl.BlockSpec(memory_space=pltpu.VMEM)] * 2,
+        out_specs=(anywhere, anywhere),
+        scratch_shapes=[pltpu.SMEM((local,), F32), dma((2,))],
+    )(pltpu.with_memory_space_constraint(out, pltpu.VMEM), pltpu.with_memory_space_constraint(out_log, pltpu.VMEM))
 
 
 def solution(mesh):

time: 48.5 us -> 43.5 us (0.90)
  local copies, waits for them, and re-layouts: 2.98 us -> 0 us
  Pallas kernels: 44.6 us -> 42.7 us
    unnamed x2 -> x0, local copies, waits for them, and re-layouts: 2.98 us -> none
    pallas_call x1 -> x2, Pallas kernels: 44.6 us -> 42.7 us  [the longest x1 41.9 us: per_device(): pl.pallas_call(functools.partial(kernel, depth, width), out_shape=(pltpu....]
where the time goes in v4:
time: 43.5 us; the launch traced here: 43.3 us
  Pallas kernels  42.7 us (98%)
  between operations  0.64 us (1%)
    pallas_call x1, Pallas kernels, per_device(): pl.pallas_call(functools.partial(kernel, depth, width), out_shape=(pltpu....  41.9 us

profile of v4, /device:TPU:0, one launch (start us, length us, event | category | flops | bytes accessed | tf_op | source)
XLA Modules:
  0.0 43.3 jit_solution(6009486115245811970)
XLA Ops:
  0.6 41.9 %shard_map.86 = (bf16[8,256,128]{2,1,0:T(8,128)(2,1)S(1)}, f32[8,128]{1,0:T(8,128)S(1)}) custom-call(bf16[8,256,128]{2,1,0:T(8,128)(2,1)} %walkers_in.1, bf16[8,128,128]{2,1,0:T(8,128)(2,1)} %inverse_in.1, bf16[512,128]{1,0:T(8,128)(2,1)} %trial_in.1, bf16[8,256,512]{2,1,0:T(8,128)(2,1)} %vectors_in.1, f32[8,8]{1,0:T(8,128)} %aux_in.1, f32[8]{0:T(128)} %log_in.1, ...), custom_call_target="tpu_custom_call" | custom-call | tf_op jit(solution)/shard_map/pallas_call | solution.py:576
  42.5 0.8 %shard_map.87 = (bf16[8,256,128]{2,1,0:T(8,128)(2,1)}, f32[8]{0:T(128)}) custom-call(bf16[8,256,128]{2,1,0:T(8,128)(2,1)S(1)} %get-tuple-element.4.out_ref, f32[8,128]{1,0:T(8,128)S(1)} %get-tuple-element.5.log_ref), custom_call_target="tpu_custom_call" | custom-call | tf_op jit(solution)/shard_map/pallas_call | solution.py:648

commit v5 on v4

--- a/solution.py
+++ b/solution.py
@@ -11,10 +11,11 @@
 ORDER = 6
 BLOCKS = 4
 SUB = 1
-SKEW = 5
-PARTS = 2
+SKEW = 4
+PARTS = 1
+LOADS = 4
 REACH = 3
-PLANS = ((2, -1, 1), (3, 2, 1), (2, 1), (2, 1))
+PLANS = ((2, -1, 1), (3, 2, 1), (3, 2, 1), (2, 1))
 MESH = pl.DeviceIdType.MESH
 F32 = jnp.float32
 BF16 = jnp.bfloat16
@@ -33,7 +34,7 @@
     walkers_in, inverse_in, trial_in, vectors_in, aux_in, log_in, copies_in,
     out, out_log,
     walkers, inverse, trial, vectors, aux, log_weight, copies,
-    green, mixed, strips, level, bias_all, facts, picked, partial, leaving, arrived, given, crossed,
+    green, mixed, strips, level, bias_all, facts, known, picked, partial, leaving, arrived, given, crossed,
     back, extra_in, extra_out, edge, staged, pool, full, term, result,
     load_sems, copies_send, copies_recv, facts_send, facts_recv, bias_send, bias_recv,
     chain_send, chain_recv, cross_recv, back_recv, swap_send, swap_recv, extra_send, extra_recv, edge_sems,
@@ -78,22 +79,34 @@
         for core in range(2):
             greet({"vec": z + 1, "orb": core})
 
-    pairs = (
-        (copies_in, copies.at[x]), (log_in, log_weight), (walkers_in, walkers), (inverse_in, inverse), (trial_in, trial),
-        (vectors_in, vectors), (aux_in, aux),
-    )
+    batch = count // LOADS
+    pairs = [
+        (inverse_in, inverse), (walkers_in, walkers), (trial_in, trial), (copies_in, copies.at[x]), (log_in, log_weight),
+        (aux_in, aux),
+    ]
+    for n in range(LOADS):
+        group = pl.ds(n * batch, batch)
+        pairs.append((vectors_in.at[group], vectors.at[group]))
     loads = [pltpu.make_async_copy(src, dst, load_sems.at[n]) for n, (src, dst) in enumerate(pairs)]
     for load in loads:
         load.start()
 
-    loads[2].wait()
-    loads[3].wait()
+    loads[0].wait()
+    loads[1].wait()
     for w in range(local):
         green[w] = jnp.dot(walkers[w], inverse[w], preferred_element_type=F32).astype(BF16)
-    loads[4].wait()
-    loads[5].wait()
-    for g in range(count):
-        mixed[g] = jnp.dot(vectors[g], trial[...], preferred_element_type=F32).astype(BF16)
+    for n in range(2, 6):
+        loads[n].wait()
+    walker_id = lax.broadcasted_iota(jnp.int32, (local, lanes), 0)
+    weights = jnp.zeros((local, lanes), F32)
+    for w in range(local):
+        weights = jnp.where(walker_id == w, log_weight[w], weights)
+    facts[x] = weights
+    facts[x, :, 0:count] = aux[...]
+    for n in range(LOADS):
+        loads[6 + n].wait()
+        for g in range(n * batch, (n + 1) * batch):
+            mixed[g] = jnp.dot(vectors[g], trial[...], preferred_element_type=F32).astype(BF16)
     gram = jnp.zeros((local * span, wide), F32)
     for j in range(rows // span):
         left = green[:, j * span:(j + 1) * span, :].reshape(local * span, electrons)
@@ -103,23 +116,13 @@
     col_id = lax.broadcasted_iota(jnp.int32, (local * span, wide), 1)
     same = row_id % span == col_id % span
     folded = jnp.sum(jnp.where(same, gram, 0.0).reshape(local, span, wide), axis=1)
-    wide_row = lax.broadcasted_iota(jnp.int32, (wide, wide), 0)
-    wide_col = lax.broadcasted_iota(jnp.int32, (wide, wide), 1)
-    groups = jnp.where(wide_row // span == wide_col // span, 1.0, 0.0).astype(F32)
-    bias_all[o, x] = jnp.dot(folded, groups, precision=lax.Precision.HIGHEST, preferred_element_type=F32)
-
-    loads[6].wait()
-    loads[0].wait()
-    loads[1].wait()
-    pick_row = lax.broadcasted_iota(jnp.int32, (count, wide), 0)
-    pick_col = lax.broadcasted_iota(jnp.int32, (count, wide), 1)
-    pick = jnp.where(pick_row == pick_col // span, 1.0, 0.0).astype(F32)
-    facts[x, 0:local, :] = jnp.dot(aux[...], pick, precision=lax.Precision.HIGHEST, preferred_element_type=F32)
-    walker_id = lax.broadcasted_iota(jnp.int32, (local, wide), 0)
-    weights = jnp.zeros((local, wide), F32)
-    for w in range(local):
-        weights = jnp.where(walker_id == w, log_weight[w], weights)
-    facts[x, local:2 * local, :] = weights
+    lane_id = lax.broadcasted_iota(jnp.int32, (local, wide), 1)
+    reach = 1
+    while reach < span:
+        low = lane_id % (2 * reach) < reach
+        folded = folded + jnp.where(low, pltpu.roll(folded, wide - reach, 1), pltpu.roll(folded, reach, 1))
+        reach *= 2
+    bias_all[o, x] = folded
 
     sides = jnp.where(z > 0, 2, 0) + jnp.where(z < last, 2, 0)
     pl.semaphore_wait(barrier, 1 + 2 * (width - 1) + sides)
@@ -129,9 +132,6 @@
         remote(bias_all.at[o, x], bias_all.at[o, x], bias_send.at[n], bias_recv.at[o, x], where)
         for n, where in enumerate(bias_peers)
     ]
-    for copy in bias_copies:
-        copy.start()
-
     def facts_copy(hop, owner):
         return remote(
             facts.at[owner], facts.at[owner], facts_send.at[hop], facts_recv.at[owner], {"walk": lax.rem(x + hop, width)}
@@ -143,9 +143,11 @@
             {"walk": lax.rem(x + hop, width)},
         )
 
+    for copy in bias_copies:
+        copy.start()
     for hop in hops:
+        facts_copy(hop, x).start()
         copies_copy(hop, x).start()
-        facts_copy(hop, x).start()
 
     chunk_row = lax.broadcasted_iota(jnp.int32, (count, span, block), 1)
     chunk_col = lax.broadcasted_iota(jnp.int32, (count, span, block), 2)
@@ -168,25 +170,27 @@
     level[...] = crossing.reshape(wide, block).astype(BF16)
 
     for hop in hops:
+        facts_copy(hop, lax.rem(x + hop, width)).wait_recv()
+    sources = [(copies[x, s] // local, pl.ds(copies[x, s] % local, 1)) for s in range(local)]
+    for s, (column, row) in enumerate(sources):
+        known[s:s + 1, :] = facts[column, row, :]
+    pick_row = lax.broadcasted_iota(jnp.int32, (count, wide), 0)
+    pick_col = lax.broadcasted_iota(jnp.int32, (count, wide), 1)
+    pick = jnp.where(pick_row == pick_col // span, 1.0, 0.0).astype(F32)
+    drawn = jnp.dot(known[:, 0:count], pick, precision=lax.Precision.HIGHEST, preferred_element_type=F32)
+    old_log = jnp.broadcast_to(known[:, count:count + 1], (local, lanes))
+
+    for hop in hops:
         other = lax.rem(x + hop, width)
-        facts_copy(hop, other).wait_recv()
         for core in range(2):
             remote(
                 bias_all.at[core, other], bias_all.at[core, other], bias_send.at[0], bias_recv.at[core, other], {"walk": other}
             ).wait_recv()
     remote(bias_all.at[1 - o, x], bias_all.at[1 - o, x], bias_send.at[0], bias_recv.at[1 - o, x], {"orb": 1 - o}).wait_recv()
 
-    for s in range(local):
-        source = copies[x, s]
-        column = source // local
-        at = source % local
-        row = pl.ds(at, 1)
-        picked[0, s:s + 1, :] = bias_all[0, column, row, :] + bias_all[1, column, row, :]
-        picked[1, s:s + 1, :] = facts[column, row, :]
-        picked[2, s:s + 1, :] = facts[column, pl.ds(local + at, 1), :]
-
-    bias = picked[0]
-    drawn = picked[1]
+    for s, (column, row) in enumerate(sources):
+        picked[s:s + 1, :] = bias_all[0, column, row, :] + bias_all[1, column, row, :]
+    bias = picked[...]
     shift = -step_root * bias
     field = drawn - shift
     factor = jnp.sum(drawn * shift - 0.5 * shift * shift, axis=1, keepdims=True) * (1.0 / span)
@@ -468,7 +472,7 @@
         def _():
             finish(a)
 
-    new_log = picked[2][:, 0:lanes] + factor + extra_in[0, 0:local, :] + extra_in[1, 0:local, :]
+    new_log = old_log + factor + extra_in[0, 0:local, :] + extra_in[1, 0:local, :]
     out_log[...] = new_log
 
     def onward(w, part, hop_to):
@@ -594,8 +598,9 @@
             pltpu.VMEM((block // span, wide, BLOCKS * block), BF16),
             pltpu.VMEM((wide, block), BF16),
             pltpu.VMEM((2, width, local, wide), F32),
-            pltpu.VMEM((width, 2 * local, wide), F32),
-            pltpu.VMEM((3, local, wide), F32),
+            pltpu.VMEM((width, local, lanes), F32),
+            pltpu.VMEM((local, lanes), F32),
+            pltpu.VMEM((local, wide), F32),
             pltpu.VMEM((local, BLOCKS, block, block), F32),
             pltpu.VMEM((2, chunks, piece, block), BF16),
             pltpu.VMEM((2, chunks, piece, block), BF16),
@@ -610,7 +615,7 @@
             pltpu.VMEM((orbitals, orbitals), BF16),
             pltpu.VMEM((orbitals, electrons), BF16),
             pltpu.VMEM((mine, 2, rows, electrons), BF16),
-            dma((7,)),
+            dma((6 + LOADS,)),
             dma((width,)),
             dma((width,)),
             dma((width,)),

time: 43.5 us -> 42 us (0.966)
  Pallas kernels: 42.7 us -> 41.2 us
    pallas_call x1, Pallas kernels: 41.9 us -> 40.4 us  [per_device(): pl.pallas_call(functools.partial(kernel, depth, width), out_shape=(pltpu....]
where the time goes in v5:
time: 42 us; the launch traced here: 41.9 us
  Pallas kernels  41.2 us (98%)
  between operations  0.64 us (2%)
    pallas_call x1, Pallas kernels, per_device(): pl.pallas_call(functools.partial(kernel, depth, width), out_shape=(pltpu....  40.4 us

profile of v5, /device:TPU:0, one launch (start us, length us, event | category | flops | bytes accessed | tf_op | source)
XLA Modules:
  0.0 41.9 jit_solution(10047850276593417171)
XLA Ops:
  0.6 40.4 %shard_map.86 = (bf16[8,256,128]{2,1,0:T(8,128)(2,1)S(1)}, f32[8,128]{1,0:T(8,128)S(1)}) custom-call(bf16[8,256,128]{2,1,0:T(8,128)(2,1)} %walkers_in.1, bf16[8,128,128]{2,1,0:T(8,128)(2,1)} %inverse_in.1, bf16[512,128]{1,0:T(8,128)(2,1)} %trial_in.1, bf16[8,256,512]{2,1,0:T(8,128)(2,1)} %vectors_in.1, f32[8,8]{1,0:T(8,128)} %aux_in.1, f32[8]{0:T(128)} %log_in.1, ...), custom_call_target="tpu_custom_call" | custom-call | tf_op jit(solution)/shard_map/pallas_call | solution.py:580
  41.0 0.8 %shard_map.87 = (bf16[8,256,128]{2,1,0:T(8,128)(2,1)}, f32[8]{0:T(128)}) custom-call(bf16[8,256,128]{2,1,0:T(8,128)(2,1)S(1)} %get-tuple-element.4.out_ref, f32[8,128]{1,0:T(8,128)S(1)} %get-tuple-element.5.log_ref), custom_call_target="tpu_custom_call" | custom-call | tf_op jit(solution)/shard_map/pallas_call | solution.py:653

commit v6 on v5

--- a/solution.py
+++ b/solution.py
@@ -12,6 +12,7 @@
 BLOCKS = 4
 SUB = 1
 SKEW = 4
+SKIPS = ()
 PARTS = 1
 LOADS = 4
 REACH = 3
@@ -38,7 +39,7 @@
     back, extra_in, extra_out, edge, staged, pool, full, term, result,
     load_sems, copies_send, copies_recv, facts_send, facts_recv, bias_send, bias_recv,
     chain_send, chain_recv, cross_recv, back_recv, swap_send, swap_recv, extra_send, extra_recv, edge_sems,
-    stage_send, pool_recv, own_send, next_send, slot_recv,
+    stage_send, pool_recv, own_send, next_send, slot_recv, write_sems,
 ):
     gathered = out
     z = lax.axis_index("vec")
@@ -57,6 +58,7 @@
     mine = half // 2
     lanes = extra_in.shape[2]
     insets = [1 if a == half - 1 and last >= REACH else 0 for a in range(half)]
+    skips = [last >= REACH and a in SKIPS and not insets[a] for a in range(half)]
     hops = range(1, width)
 
     barrier = pltpu.get_barrier_semaphore()
@@ -69,15 +71,16 @@
         for core in range(2):
             greet({"walk": lax.rem(x + hop, width), "orb": core})
 
-    @pl.when(z > 0)
-    def _():
-        for core in range(2):
-            greet({"vec": z - 1, "orb": core})
-
-    @pl.when(z < last)
-    def _():
-        for core in range(2):
-            greet({"vec": z + 1, "orb": core})
+    for hop in (1, 2):
+        @pl.when(z >= hop)
+        def _():
+            for core in range(2):
+                greet({"vec": z - hop, "orb": core})
+
+        @pl.when(z <= last - hop)
+        def _():
+            for core in range(2):
+                greet({"vec": z + hop, "orb": core})
 
     batch = count // LOADS
     pairs = [
@@ -107,11 +110,11 @@
         loads[6 + n].wait()
         for g in range(n * batch, (n + 1) * batch):
             mixed[g] = jnp.dot(vectors[g], trial[...], preferred_element_type=F32).astype(BF16)
-    gram = jnp.zeros((local * span, wide), F32)
-    for j in range(rows // span):
-        left = green[:, j * span:(j + 1) * span, :].reshape(local * span, electrons)
-        right = mixed[:, j * span:(j + 1) * span, :].reshape(wide, electrons)
-        gram = gram + lax.dot_general(left, right, (((1,), (1,)), ((), ())), preferred_element_type=F32)
+    left = [green[:, j * span:(j + 1) * span, :].reshape(local * span, electrons) for j in range(rows // span)]
+    right = [mixed[:, j * span:(j + 1) * span, :].reshape(wide, electrons) for j in range(rows // span)]
+    gram = lax.dot_general(
+        jnp.concatenate(left, axis=1), jnp.concatenate(right, axis=1), (((1,), (1,)), ((), ())), preferred_element_type=F32
+    )
     row_id = lax.broadcasted_iota(jnp.int32, (local * span, wide), 0)
     col_id = lax.broadcasted_iota(jnp.int32, (local * span, wide), 1)
     same = row_id % span == col_id % span
@@ -124,7 +127,7 @@
         reach *= 2
     bias_all[o, x] = folded
 
-    sides = jnp.where(z > 0, 2, 0) + jnp.where(z < last, 2, 0)
+    sides = sum(jnp.where(z >= hop, 2, 0) + jnp.where(z <= last - hop, 2, 0) for hop in (1, 2))
     pl.semaphore_wait(barrier, 1 + 2 * (width - 1) + sides)
 
     bias_peers = [{"walk": lax.rem(x + hop, width), "orb": core} for hop in hops for core in range(2)] + [{"orb": 1 - o}]
@@ -205,7 +208,12 @@
             partial[:, n, j * span:(j + 1) * span, :] = summed[:, n * block:(n + 1) * block].reshape(local, span, block)
     edge_part = jnp.dot(weighted, level[...], preferred_element_type=F32)
 
-    to_next = [z - 1, z + 1]
+    def to_next(side):
+        return jnp.where(side == 0, z - 1, z + 1)
+
+    def to_far(side):
+        return jnp.where(side == 0, z - 2, z + 2)
+
     upstream = [last - z, z]
     downstream = [z, last - z]
     at_end = (z == 0) | (z == last)
@@ -217,29 +225,36 @@
     def depth_of(c):
         return sum(jnp.where(c // each == a, n, 0) for a, n in enumerate(insets) if n) + jnp.int32(0)
 
-    def chain_copy(side, c):
-        return remote(
-            leaving.at[side, c], arrived.at[side, c], chain_send.at[side, c], chain_recv.at[side, c],
-            {"vec": to_next[side]},
-        )
-
-    def cross_copy(side, c):
-        return remote(
-            leaving.at[side, c], crossed.at[c], chain_send.at[side, c], cross_recv.at[c],
-            {"vec": to_next[side], "orb": 1 - o},
+    def skip_of(c):
+        return functools.reduce(jnp.logical_or, [c // each == a for a in range(half) if skips[a]], jnp.bool_(False))
+
+    def chain_copy(side, c, hop=to_next):
+        return remote(
+            leaving.at[side, c], arrived.at[side, c], chain_send.at[side, c // each], chain_recv.at[side, c], {"vec": hop(side)}
+        )
+
+    def cross_copy(side, c, hop=to_next):
+        return remote(
+            leaving.at[side, c], crossed.at[c], chain_send.at[side, c // each], cross_recv.at[c // (2 * each) * each + c % each], {"vec": hop(side), "orb": 1 - o}
+        )
+
+    def raw_copy(side, c):
+        return remote(
+            leaving.at[side, c], back.at[o, c], chain_send.at[side, c // each], back_recv.at[o, c // (2 * each)],
+            {"vec": to_next(side), "orb": (c // each) % 2},
         )
 
     def swap_copy(c):
-        return remote(leaving.at[near, c], given.at[c], swap_send.at[c], swap_recv.at[c], {"orb": 1 - o})
+        return remote(leaving.at[near, c], given.at[c], swap_send.at[c // (2 * each)], swap_recv.at[c // (2 * each)], {"orb": 1 - o})
 
     def extra_copy(side):
         return remote(
-            extra_out.at[side], extra_in.at[side], extra_send.at[side], extra_recv.at[side], {"vec": to_next[side]}
+            extra_out.at[side], extra_in.at[side], extra_send.at[side], extra_recv.at[side], {"vec": to_next(side)}
         )
 
     def back_copy(c):
         return remote(
-            leaving.at[near, c], back.at[o, c], chain_send.at[near, c], back_recv.at[o, c],
+            leaving.at[near, c], back.at[o, c], chain_send.at[near, c // each], back_recv.at[o, c // (2 * each)],
             {"vec": inward, "orb": (c // each) % 2},
         )
 
@@ -248,12 +263,16 @@
         return partial[side * half + c // each, at // SUB, pl.ds(pl.multiple_of((at % SUB) * piece, piece), piece), :]
 
     def chain_step(t, carry):
-        for side in range(2):
-            c = t - SKEW * upstream[side]
-            head = upstream[side] == 0
-            togo = downstream[side] - depth_of(c)
-
-            @pl.when((c >= 0) & (c < chunks) & (togo > 0))
+        for turn in range(2):
+            side = jnp.where(z <= last - z, 1 - turn, turn)
+            before = jnp.where(side == 0, last - z, z)
+            after = last - before
+            c = t - SKEW * before
+            head = before == 0
+            togo = after - depth_of(c)
+            skip = skip_of(c)
+
+            @pl.when((c >= 0) & (c < chunks) & ((togo > 1) | ((togo == 1) & jnp.logical_not(skip))))
             def _():
                 own = part_of(side, c)
                 here = (c // each) % 2 == o
@@ -267,7 +286,9 @@
                     chain_copy(side, c).wait_recv()
                     leaving[side, c] = (own + arrived[side, c].astype(F32)).astype(BF16)
 
-                @pl.when((togo > 1) | here)
+                jump = skip & (togo == 2)
+
+                @pl.when(jnp.logical_not(jump) & ((togo > 1) | here))
                 def _():
                     chain_copy(side, c).start()
 
@@ -275,21 +296,41 @@
                 def _():
                     cross_copy(side, c).start()
 
-                @pl.when(c == 0)
+                @pl.when(jump & here)
                 def _():
-                    @pl.when(head)
-                    def _():
-                        extra_in[side] = jnp.zeros_like(extra_in[side])
-
-                    @pl.when(jnp.logical_not(head))
-                    def _():
-                        extra_copy(side).wait_recv()
-
-                    extra_out[side, 0:local, :] = extra_in[side, 0:local, :] + factor
-                    extra_out[side, local:, :] = extra_in[side, local:, :] + edge_part
-                    extra_copy(side).start()
+                    chain_copy(side, c, to_far).start()
+
+                @pl.when(jump & jnp.logical_not(here))
+                def _():
+                    cross_copy(side, c, to_far).start()
+
+            @pl.when((c == 0) & (after > 0))
+            def _():
+                @pl.when(head)
+                def _():
+                    extra_in[side] = jnp.zeros_like(extra_in[side])
+
+                @pl.when(jnp.logical_not(head))
+                def _():
+                    extra_copy(side).wait_recv()
+
+                extra_out[side, 0:local, :] = extra_in[side, 0:local, :] + factor
+                extra_out[side, local:, :] = extra_in[side, local:, :] + edge_part
+                extra_copy(side).start()
 
         return carry
+
+    for side in range(2):
+        @pl.when(downstream[side] == 1)
+        def _():
+            def raw_step(c, carry):
+                leaving[side, c] = part_of(side, c).astype(BF16)
+                raw_copy(side, c).start()
+                return carry
+
+            for a in range(half):
+                if skips[a]:
+                    lax.fori_loop(a * each, (a + 1) * each, raw_step, jnp.int32(0))
 
     lax.fori_loop(0, SKEW * (last - 1) + chunks, chain_step, jnp.int32(0))
 
@@ -401,27 +442,28 @@
         def put(r, c, value):
             full[columns(r), columns(c)] = value
 
+        whole = pl.ds(a * each, each)
+        remote(leaving.at[near, whole], given.at[whole], swap_send.at[i], swap_recv.at[i], {"orb": 1 - o}).wait_recv()
+        if insets[a] or skips[a]:
+            for core in range(2):
+                remote(
+                    leaving.at[near, whole], back.at[core, whole], chain_send.at[near, a], back_recv.at[core, i],
+                    {"vec": inward, "orb": core},
+                ).wait_recv()
         for n in range(BLOCKS):
             first_c = a * each + n * SUB
             for c in range(first_c, first_c + SUB):
                 remote(
-                    leaving.at[near, c], arrived.at[near, c], chain_send.at[near, c], chain_recv.at[near, c], {"vec": inward}
+                    leaving.at[near, c], arrived.at[near, c], chain_send.at[near, c // each], chain_recv.at[near, c], {"vec": inward}
                 ).wait_recv()
-                swap_copy(c).wait_recv()
                 remote(
-                    leaving.at[near, c], crossed.at[c], chain_send.at[near, c], cross_recv.at[c],
+                    leaving.at[near, c], crossed.at[c], chain_send.at[near, c // each], cross_recv.at[c // (2 * each) * each + c % each],
                     {"vec": inward, "orb": 1 - o},
                 ).wait_recv()
-                if insets[a]:
-                    for core in range(2):
-                        remote(
-                            leaving.at[near, c], back.at[core, c], chain_send.at[near, c], back_recv.at[core, c],
-                            {"vec": away_z(-1), "orb": core},
-                        ).wait_recv()
             run = pl.ds(first_c, SUB)
             kept = partial[w, n] + arrived[near, run].reshape(block, block).astype(F32)
             taken = given[run].reshape(block, block).astype(F32) + crossed[run].reshape(block, block).astype(F32)
-            if insets[a]:
+            if insets[a] or skips[a]:
                 kept = kept + back[o, run].reshape(block, block).astype(F32)
                 taken = taken + back[1 - o, run].reshape(block, block).astype(F32)
             for core, value in ((o, kept), (1 - o, taken)):
@@ -465,7 +507,8 @@
         result[i] = running.astype(BF16).reshape(2, rows, electrons)
         for copy in spread_copies(a):
             copy.start()
-        gathered[w] = result[i, o]
+        settle = pltpu.make_async_copy(result.at[i, o], gathered.at[w], write_sems.at[i])
+        settle.start()
 
     for a in range(half):
         @pl.when(at_owner[a] & (a % 2 == o))
@@ -489,15 +532,11 @@
         for side in (near, 1 - near):
             w, away, hop_to = route(side, a)
 
-            @pl.when((away != 0) | (o != a % 2))
+            @pl.when(passes(a, away))
             def _():
                 for part in range(PARTS):
                     onward(w, part, hop_to).wait_recv()
-
-                    @pl.when(passes(a, away))
-                    def _():
-                        onward(w, part, hop_to).start()
-
+                    onward(w, part, hop_to).start()
 
     for copy in bias_copies:
         copy.wait_send()
@@ -505,15 +544,18 @@
         facts_copy(hop, x).wait_send()
         copies_copy(hop, x).wait_send()
 
-    def drain(c, carry):
-        for side in range(2):
-            @pl.when(downstream[side] - depth_of(c) > 0)
-            def _():
-                chain_copy(side, c).wait_send()
-
-        return carry
-
-    lax.fori_loop(0, chunks, drain, jnp.int32(0))
+    def sent(side, a):
+        whole = pl.ds(a * each, each)
+        return remote(
+            leaving.at[side, whole], arrived.at[side, whole], chain_send.at[side, a], chain_recv.at[side, a], {"orb": 1 - o}
+        )
+
+    for side in range(2):
+        for a in range(half):
+            @pl.when(downstream[side] - insets[a] != 0)
+            def _():
+                sent(side, a).wait_send()
+
     for side in range(2):
         @pl.when(downstream[side] > 0)
         def _():
@@ -533,25 +575,26 @@
             def _():
                 stage_copy(0, a).wait_send()
 
-                def taken_back(c, carry):
-                    swap_copy(c).wait_send()
-                    return carry
-
-                lax.fori_loop(a * each, (a + 1) * each, taken_back, jnp.int32(0))
-
-            @pl.when(a % 2 == o)
-            def _():
-                for copy in spread_copies(a):
-                    copy.wait_send()
-
-        if insets[a]:
-            @pl.when(at_end)
-            def _():
-                def back_done(c, carry):
-                    back_copy(c).wait_send()
-                    return carry
-
-                lax.fori_loop(a * each, (a + 1) * each, back_done, jnp.int32(0))
+                whole = pl.ds(a * each, each)
+                remote(
+                    leaving.at[near, whole], given.at[whole], swap_send.at[a // 2], swap_recv.at[a // 2], {"orb": 1 - o}
+                ).wait_send()
+
+    for a in range(half):
+        for side in (near, 1 - near):
+            w, away, hop_to = route(side, a)
+
+            @pl.when(((away != 0) | (o != a % 2)) & jnp.logical_not(passes(a, away)))
+            def _():
+                for part in range(PARTS):
+                    onward(w, part, hop_to).wait_recv()
+
+    for a in range(half):
+        @pl.when(at_owner[a] & (a % 2 == o))
+        def _():
+            for copy in spread_copies(a):
+                copy.wait_send()
+            pltpu.make_async_copy(result.at[a // 2, o], gathered.at[base + a], write_sems.at[a // 2]).wait()
 
     for a in range(half):
         for side in range(2):
@@ -584,7 +627,7 @@
             pltpu.VMEM((local, 128), F32),
         ),
         in_specs=[anywhere] * 7,
-        out_specs=(pl.BlockSpec(memory_space=pltpu.VMEM), pl.BlockSpec(memory_space=pltpu.VMEM)),
+        out_specs=(anywhere, pl.BlockSpec(memory_space=pltpu.VMEM)),
         scratch_shapes=[
             pltpu.VMEM(walkers.shape, BF16),
             pltpu.VMEM(inv_intersection.shape, BF16),
@@ -622,12 +665,12 @@
             dma((width,)),
             dma((2 * width,)),
             dma((2, width)),
+            dma((2, half)),
             dma((2, chunks)),
-            dma((2, chunks)),
-            dma((chunks,)),
-            dma((2, chunks)),
-            dma((chunks,)),
-            dma((chunks,)),
+            dma((chunks // 2,)),
+            dma((2, mine)),
+            dma((mine,)),
+            dma((mine,)),
             dma((2,)),
             dma((2,)),
             dma((2,)),
@@ -636,6 +679,7 @@
             dma((mine, 2 * reach + 1, PARTS)),
             dma((local, PARTS)),
             dma((local, PARTS)),
+            dma((mine,)),
         ],
         compiler_params=pltpu.CompilerParams(collective_id=0, has_side_effects=True),
     )(walkers, inv_intersection, trial, vectors, aux_field, log_weight, copy_list)

time: 42 us -> 40.1 us (0.955)
  Pallas kernels: 41.2 us -> 39.3 us
    pallas_call x1, Pallas kernels: 40.4 us -> 38.5 us  [per_device(): pl.pallas_call(functools.partial(kernel, depth, width), out_shape=(pltpu....]
where the time goes in v6:
time: 40.1 us; the launch traced here: 40 us
  Pallas kernels  39.3 us (98%)
  between operations  0.64 us (2%)
    pallas_call x1, Pallas kernels, per_device(): pl.pallas_call(functools.partial(kernel, depth, width), out_shape=(pltpu....  38.5 us
    pallas_call x1, Pallas kernels, per_device(): pl.pallas_call(settle, out_shape=(jax.ShapeDtypeStruct(walkers.shape, BF1...  0.82 us

profile of v6, /device:TPU:0, one launch (start us, length us, event | category | flops | bytes accessed | tf_op | source)
XLA Modules:
  0.0 40.0 jit_solution(7319620727611886544)
XLA Ops:
  0.6 38.5 %shard_map.86 = (bf16[8,256,128]{2,1,0:T(8,128)(2,1)S(1)}, f32[8,128]{1,0:T(8,128)S(1)}) custom-call(bf16[8,256,128]{2,1,0:T(8,128)(2,1)} %walkers_in.1, bf16[8,128,128]{2,1,0:T(8,128)(2,1)} %inverse_in.1, bf16[512,128]{1,0:T(8,128)(2,1)} %trial_in.1, bf16[8,256,512]{2,1,0:T(8,128)(2,1)} %vectors_in.1, f32[8,8]{1,0:T(8,128)} %aux_in.1, f32[8]{0:T(128)} %log_in.1, ...), custom_call_target="tpu_custom_call" | custom-call | tf_op jit(solution)/shard_map/pallas_call | solution.py:623
  39.2 0.8 %shard_map.87 = (bf16[8,256,128]{2,1,0:T(8,128)(2,1)}, f32[8]{0:T(128)}) custom-call(bf16[8,256,128]{2,1,0:T(8,128)(2,1)S(1)} %get-tuple-element.4.out_ref, f32[8,128]{1,0:T(8,128)S(1)} %get-tuple-element.5.log_ref), custom_call_target="tpu_custom_call" | custom-call | tf_op jit(solution)/shard_map/pallas_call | solution.py:697

commit v7 on v6

--- a/solution.py
+++ b/solution.py
@@ -36,7 +36,7 @@
     out, out_log,
     walkers, inverse, trial, vectors, aux, log_weight, copies,
     green, mixed, strips, level, bias_all, facts, known, picked, partial, leaving, arrived, given, crossed,
-    back, extra_in, extra_out, edge, staged, pool, full, term, result,
+    back, extra_in, extra_out, edge, staged, pool, full, terms, result,
     load_sems, copies_send, copies_recv, facts_send, facts_recv, bias_send, bias_recv,
     chain_send, chain_recv, cross_recv, back_recv, swap_send, swap_recv, extra_send, extra_recv, edge_sems,
     stage_send, pool_recv, own_send, next_send, slot_recv, write_sems,
@@ -71,7 +71,7 @@
         for core in range(2):
             greet({"walk": lax.rem(x + hop, width), "orb": core})
 
-    for hop in (1, 2):
+    for hop in (1,):
         @pl.when(z >= hop)
         def _():
             for core in range(2):
@@ -83,33 +83,32 @@
                 greet({"vec": z + hop, "orb": core})
 
     batch = count // LOADS
-    pairs = [
-        (inverse_in, inverse), (walkers_in, walkers), (trial_in, trial), (copies_in, copies.at[x]), (log_in, log_weight),
-        (aux_in, aux),
-    ]
+    pairs = [(trial_in, trial)]
     for n in range(LOADS):
         group = pl.ds(n * batch, batch)
         pairs.append((vectors_in.at[group], vectors.at[group]))
+    pairs += [
+        (inverse_in, inverse), (walkers_in, walkers), (copies_in, copies.at[x]), (log_in, log_weight), (aux_in, aux),
+    ]
     loads = [pltpu.make_async_copy(src, dst, load_sems.at[n]) for n, (src, dst) in enumerate(pairs)]
     for load in loads:
         load.start()
 
     loads[0].wait()
-    loads[1].wait()
+    for n in range(LOADS):
+        loads[1 + n].wait()
+        for g in range(n * batch, (n + 1) * batch):
+            mixed[g] = jnp.dot(vectors[g], trial[...], preferred_element_type=F32).astype(BF16)
+    for load in loads[1 + LOADS:]:
+        load.wait()
     for w in range(local):
         green[w] = jnp.dot(walkers[w], inverse[w], preferred_element_type=F32).astype(BF16)
-    for n in range(2, 6):
-        loads[n].wait()
     walker_id = lax.broadcasted_iota(jnp.int32, (local, lanes), 0)
     weights = jnp.zeros((local, lanes), F32)
     for w in range(local):
         weights = jnp.where(walker_id == w, log_weight[w], weights)
     facts[x] = weights
     facts[x, :, 0:count] = aux[...]
-    for n in range(LOADS):
-        loads[6 + n].wait()
-        for g in range(n * batch, (n + 1) * batch):
-            mixed[g] = jnp.dot(vectors[g], trial[...], preferred_element_type=F32).astype(BF16)
     left = [green[:, j * span:(j + 1) * span, :].reshape(local * span, electrons) for j in range(rows // span)]
     right = [mixed[:, j * span:(j + 1) * span, :].reshape(wide, electrons) for j in range(rows // span)]
     gram = lax.dot_general(
@@ -127,7 +126,7 @@
         reach *= 2
     bias_all[o, x] = folded
 
-    sides = sum(jnp.where(z >= hop, 2, 0) + jnp.where(z <= last - hop, 2, 0) for hop in (1, 2))
+    sides = sum(jnp.where(z >= hop, 2, 0) + jnp.where(z <= last - hop, 2, 0) for hop in (1,))
     pl.semaphore_wait(barrier, 1 + 2 * (width - 1) + sides)
 
     bias_peers = [{"walk": lax.rem(x + hop, width), "orb": core} for hop in hops for core in range(2)] + [{"orb": 1 - o}]
@@ -442,6 +441,25 @@
         def put(r, c, value):
             full[columns(r), columns(c)] = value
 
+        for hop in range(width):
+            other = lax.rem(x + hop, width)
+            for core in range(2):
+                arrival = remote(
+                    staged.at[0, 0], pool.at[other, i, core], stage_send.at[0, 0], pool_recv.at[other, i, core],
+                    {"walk": other, "orb": core},
+                )
+                if hop > 0:
+                    arrival.wait_recv()
+                else:
+                    @pl.when(core != o)
+                    def _():
+                        arrival.wait_recv()
+        column = copies[x, w] // local
+        for core in range(2):
+            start = pool[0, i, core]
+            for other in hops:
+                start = jnp.where(column == other, pool[other, i, core], start)
+            terms[0, :, core * rows:(core + 1) * rows] = start.T
         whole = pl.ds(a * each, each)
         remote(leaving.at[near, whole], given.at[whole], swap_send.at[i], swap_recv.at[i], {"orb": 1 - o}).wait_recv()
         if insets[a] or skips[a]:
@@ -479,32 +497,13 @@
                     put(r, k, value)
                     put(k, r, value.T)
 
-        for hop in range(width):
-            other = lax.rem(x + hop, width)
-            for core in range(2):
-                arrival = remote(
-                    staged.at[0, 0], pool.at[other, i, core], stage_send.at[0, 0], pool_recv.at[other, i, core],
-                    {"walk": other, "orb": core},
-                )
-                if hop > 0:
-                    arrival.wait_recv()
-                else:
-                    @pl.when(core != o)
-                    def _():
-                        arrival.wait_recv()
-        column = copies[x, w] // local
-        for core in range(2):
-            start = pool[0, i, core]
-            for other in hops:
-                start = jnp.where(column == other, pool[other, i, core], start)
-            term[core * rows:(core + 1) * rows, :] = start
-        running = term[...].astype(F32)
         for degree in range(1, ORDER + 1):
-            fresh = (jnp.dot(full[...], term[...], preferred_element_type=F32) * (1.0 / degree)).astype(BF16)
-            running = running + fresh.astype(F32)
-            if degree < ORDER:
-                term[...] = fresh
-        result[i] = running.astype(BF16).reshape(2, rows, electrons)
+            fresh = (jnp.dot(terms[degree - 1], full[...], preferred_element_type=F32) * (1.0 / degree)).astype(BF16)
+            terms[degree] = fresh
+        running = terms[0].astype(F32)
+        for degree in range(1, ORDER + 1):
+            running = running + terms[degree].astype(F32)
+        result[i] = running.astype(BF16).T.reshape(2, rows, electrons)
         for copy in spread_copies(a):
             copy.start()
         settle = pltpu.make_async_copy(result.at[i, o], gathered.at[w], write_sems.at[i])
@@ -656,7 +655,7 @@
             pltpu.VMEM((width, half, rows, electrons), BF16),
             pltpu.VMEM((width, mine, 2, rows, electrons), BF16),
             pltpu.VMEM((orbitals, orbitals), BF16),
-            pltpu.VMEM((orbitals, electrons), BF16),
+            pltpu.VMEM((ORDER + 1, electrons, orbitals), BF16),
             pltpu.VMEM((mine, 2, rows, electrons), BF16),
             dma((6 + LOADS,)),
             dma((width,)),

time: 40.1 us -> 39.4 us (0.983); the launches traced: 40 us -> 38.7 us
  Pallas kernels: 39.3 us -> 38.1 us
    pallas_call x1, Pallas kernels: 38.5 us -> 37.3 us  [per_device(): pl.pallas_call(functools.partial(kernel, depth, width), out_shape=(pltpu....]
where the time goes in v7:
time: 39.4 us; the launch traced here: 38.7 us
  Pallas kernels  38.1 us (97%)
  between operations  0.64 us (2%)
    pallas_call x1, Pallas kernels, per_device(): pl.pallas_call(functools.partial(kernel, depth, width), out_shape=(pltpu....  37.3 us
    pallas_call x1, Pallas kernels, per_device(): pl.pallas_call(settle, out_shape=(jax.ShapeDtypeStruct(walkers.shape, BF1...  0.82 us

profile of v7, /device:TPU:0, one launch (start us, length us, event | category | flops | bytes accessed | tf_op | source)
XLA Modules:
  0.0 38.7 jit_solution(7818125645644381661)
XLA Ops:
  0.6 37.3 %shard_map.86 = (bf16[8,256,128]{2,1,0:T(8,128)(2,1)S(1)}, f32[8,128]{1,0:T(8,128)S(1)}) custom-call(bf16[8,256,128]{2,1,0:T(8,128)(2,1)} %walkers_in.1, bf16[8,128,128]{2,1,0:T(8,128)(2,1)} %inverse_in.1, bf16[512,128]{1,0:T(8,128)(2,1)} %trial_in.1, bf16[8,256,512]{2,1,0:T(8,128)(2,1)} %vectors_in.1, f32[8,8]{1,0:T(8,128)} %aux_in.1, f32[8]{0:T(128)} %log_in.1, ...), custom_call_target="tpu_custom_call" | custom-call | tf_op jit(solution)/shard_map/pallas_call | solution.py:622
  37.9 0.8 %shard_map.87 = (bf16[8,256,128]{2,1,0:T(8,128)(2,1)}, f32[8]{0:T(128)}) custom-call(bf16[8,256,128]{2,1,0:T(8,128)(2,1)S(1)} %get-tuple-element.4.out_ref, f32[8,128]{1,0:T(8,128)S(1)} %get-tuple-element.5.log_ref), custom_call_target="tpu_custom_call" | custom-call | tf_op jit(solution)/shard_map/pallas_call | solution.py:696

commit v8 on v7

--- a/solution.py
+++ b/solution.py
@@ -12,9 +12,9 @@
 BLOCKS = 4
 SUB = 1
 SKEW = 4
-SKIPS = ()
+EARLY = 1
 PARTS = 1
-LOADS = 4
+LOADS = 2
 REACH = 3
 PLANS = ((2, -1, 1), (3, 2, 1), (3, 2, 1), (2, 1))
 MESH = pl.DeviceIdType.MESH
@@ -58,7 +58,6 @@
     mine = half // 2
     lanes = extra_in.shape[2]
     insets = [1 if a == half - 1 and last >= REACH else 0 for a in range(half)]
-    skips = [last >= REACH and a in SKIPS and not insets[a] for a in range(half)]
     hops = range(1, width)
 
     barrier = pltpu.get_barrier_semaphore()
@@ -71,16 +70,15 @@
         for core in range(2):
             greet({"walk": lax.rem(x + hop, width), "orb": core})
 
-    for hop in (1,):
-        @pl.when(z >= hop)
-        def _():
-            for core in range(2):
-                greet({"vec": z - hop, "orb": core})
-
-        @pl.when(z <= last - hop)
-        def _():
-            for core in range(2):
-                greet({"vec": z + hop, "orb": core})
+    @pl.when(z > 0)
+    def _():
+        for core in range(2):
+            greet({"vec": z - 1, "orb": core})
+
+    @pl.when(z < last)
+    def _():
+        for core in range(2):
+            greet({"vec": z + 1, "orb": core})
 
     batch = count // LOADS
     pairs = [(trial_in, trial)]
@@ -119,14 +117,16 @@
     same = row_id % span == col_id % span
     folded = jnp.sum(jnp.where(same, gram, 0.0).reshape(local, span, wide), axis=1)
     lane_id = lax.broadcasted_iota(jnp.int32, (local, wide), 1)
-    reach = 1
-    while reach < span:
-        low = lane_id % (2 * reach) < reach
-        folded = folded + jnp.where(low, pltpu.roll(folded, wide - reach, 1), pltpu.roll(folded, reach, 1))
-        reach *= 2
-    bias_all[o, x] = folded
-
-    sides = sum(jnp.where(z >= hop, 2, 0) + jnp.where(z <= last - hop, 2, 0) for hop in (1,))
+    step = 1
+    while step < span:
+        low = lane_id % (2 * step) < step
+        folded = folded + jnp.where(low, pltpu.roll(folded, wide - step, 1), pltpu.roll(folded, step, 1))
+        step *= 2
+    lane = lax.broadcasted_iota(jnp.int32, (local, lanes), 1) % span
+    fold = span // 2
+    bias_all[o, x] = jnp.where(lane < fold, folded[:, :lanes], folded[:, lanes:])
+
+    sides = jnp.where(z > 0, 2, 0) + jnp.where(z < last, 2, 0)
     pl.semaphore_wait(barrier, 1 + 2 * (width - 1) + sides)
 
     bias_peers = [{"walk": lax.rem(x + hop, width), "orb": core} for hop in hops for core in range(2)] + [{"orb": 1 - o}]
@@ -192,7 +192,11 @@
 
     for s, (column, row) in enumerate(sources):
         picked[s:s + 1, :] = bias_all[0, column, row, :] + bias_all[1, column, row, :]
-    bias = picked[...]
+    both = picked[...]
+    bias = jnp.concatenate(
+        [jnp.where(lane < fold, both, pltpu.roll(both, fold, 1)), jnp.where(lane < fold, pltpu.roll(both, lanes - fold, 1), both)],
+        axis=1,
+    )
     shift = -step_root * bias
     field = drawn - shift
     factor = jnp.sum(drawn * shift - 0.5 * shift * shift, axis=1, keepdims=True) * (1.0 / span)
@@ -210,9 +214,6 @@
     def to_next(side):
         return jnp.where(side == 0, z - 1, z + 1)
 
-    def to_far(side):
-        return jnp.where(side == 0, z - 2, z + 2)
-
     upstream = [last - z, z]
     downstream = [z, last - z]
     at_end = (z == 0) | (z == last)
@@ -224,23 +225,14 @@
     def depth_of(c):
         return sum(jnp.where(c // each == a, n, 0) for a, n in enumerate(insets) if n) + jnp.int32(0)
 
-    def skip_of(c):
-        return functools.reduce(jnp.logical_or, [c // each == a for a in range(half) if skips[a]], jnp.bool_(False))
-
-    def chain_copy(side, c, hop=to_next):
-        return remote(
-            leaving.at[side, c], arrived.at[side, c], chain_send.at[side, c // each], chain_recv.at[side, c], {"vec": hop(side)}
-        )
-
-    def cross_copy(side, c, hop=to_next):
-        return remote(
-            leaving.at[side, c], crossed.at[c], chain_send.at[side, c // each], cross_recv.at[c // (2 * each) * each + c % each], {"vec": hop(side), "orb": 1 - o}
-        )
-
-    def raw_copy(side, c):
-        return remote(
-            leaving.at[side, c], back.at[o, c], chain_send.at[side, c // each], back_recv.at[o, c // (2 * each)],
-            {"vec": to_next(side), "orb": (c // each) % 2},
+    def chain_copy(side, c):
+        return remote(
+            leaving.at[side, c], arrived.at[side, c], chain_send.at[side, c // each], chain_recv.at[side, c], {"vec": to_next(side)}
+        )
+
+    def cross_copy(side, c):
+        return remote(
+            leaving.at[side, c], crossed.at[c], chain_send.at[side, c // each], cross_recv.at[c // (2 * each) * each + c % each], {"vec": to_next(side), "orb": 1 - o}
         )
 
     def swap_copy(c):
@@ -269,9 +261,8 @@
             c = t - SKEW * before
             head = before == 0
             togo = after - depth_of(c)
-            skip = skip_of(c)
-
-            @pl.when((c >= 0) & (c < chunks) & ((togo > 1) | ((togo == 1) & jnp.logical_not(skip))))
+
+            @pl.when((c >= 0) & (c < chunks) & (togo > 0))
             def _():
                 own = part_of(side, c)
                 here = (c // each) % 2 == o
@@ -285,9 +276,7 @@
                     chain_copy(side, c).wait_recv()
                     leaving[side, c] = (own + arrived[side, c].astype(F32)).astype(BF16)
 
-                jump = skip & (togo == 2)
-
-                @pl.when(jnp.logical_not(jump) & ((togo > 1) | here))
+                @pl.when((togo > 1) | here)
                 def _():
                     chain_copy(side, c).start()
 
@@ -295,14 +284,6 @@
                 def _():
                     cross_copy(side, c).start()
 
-                @pl.when(jump & here)
-                def _():
-                    chain_copy(side, c, to_far).start()
-
-                @pl.when(jump & jnp.logical_not(here))
-                def _():
-                    cross_copy(side, c, to_far).start()
-
             @pl.when((c == 0) & (after > 0))
             def _():
                 @pl.when(head)
@@ -319,18 +300,6 @@
 
         return carry
 
-    for side in range(2):
-        @pl.when(downstream[side] == 1)
-        def _():
-            def raw_step(c, carry):
-                leaving[side, c] = part_of(side, c).astype(BF16)
-                raw_copy(side, c).start()
-                return carry
-
-            for a in range(half):
-                if skips[a]:
-                    lax.fori_loop(a * each, (a + 1) * each, raw_step, jnp.int32(0))
-
     lax.fori_loop(0, SKEW * (last - 1) + chunks, chain_step, jnp.int32(0))
 
     for hop in hops:
@@ -338,7 +307,7 @@
 
     def stage_copy(hop, a):
         return remote(
-            staged.at[hop, a], pool.at[x, a // 2, o], stage_send.at[hop, a], pool_recv.at[x, a // 2, o],
+            staged.at[hop, a], pool.at[x, a // 2, o], stage_send.at[a], pool_recv.at[a // 2],
             {"walk": lax.rem(x + hop, width), "orb": a % 2},
         )
 
@@ -425,7 +394,7 @@
         return [
             remote(
                 result.at[a // 2, core, pl.ds(part * share, share)], place(w, part),
-                own_send.at[a // 2, n, part], slot_recv.at[w, part], where,
+                own_send.at[a // 2], slot_recv.at[w, part], where,
             )
             for n, (core, where) in enumerate(targets)
             for part in range(PARTS)
@@ -441,19 +410,8 @@
         def put(r, c, value):
             full[columns(r), columns(c)] = value
 
-        for hop in range(width):
-            other = lax.rem(x + hop, width)
-            for core in range(2):
-                arrival = remote(
-                    staged.at[0, 0], pool.at[other, i, core], stage_send.at[0, 0], pool_recv.at[other, i, core],
-                    {"walk": other, "orb": core},
-                )
-                if hop > 0:
-                    arrival.wait_recv()
-                else:
-                    @pl.when(core != o)
-                    def _():
-                        arrival.wait_recv()
+        come = gathered.at[pl.ds(0, 2 * width - 1)]
+        remote(come, come, stage_send.at[0], pool_recv.at[i], {"orb": 1 - o}).wait_recv()
         column = copies[x, w] // local
         for core in range(2):
             start = pool[0, i, core]
@@ -462,7 +420,7 @@
             terms[0, :, core * rows:(core + 1) * rows] = start.T
         whole = pl.ds(a * each, each)
         remote(leaving.at[near, whole], given.at[whole], swap_send.at[i], swap_recv.at[i], {"orb": 1 - o}).wait_recv()
-        if insets[a] or skips[a]:
+        if insets[a]:
             for core in range(2):
                 remote(
                     leaving.at[near, whole], back.at[core, whole], chain_send.at[near, a], back_recv.at[core, i],
@@ -481,7 +439,7 @@
             run = pl.ds(first_c, SUB)
             kept = partial[w, n] + arrived[near, run].reshape(block, block).astype(F32)
             taken = given[run].reshape(block, block).astype(F32) + crossed[run].reshape(block, block).astype(F32)
-            if insets[a] or skips[a]:
+            if insets[a]:
                 kept = kept + back[o, run].reshape(block, block).astype(F32)
                 taken = taken + back[1 - o, run].reshape(block, block).astype(F32)
             for core, value in ((o, kept), (1 - o, taken)):
@@ -509,14 +467,6 @@
         settle = pltpu.make_async_copy(result.at[i, o], gathered.at[w], write_sems.at[i])
         settle.start()
 
-    for a in range(half):
-        @pl.when(at_owner[a] & (a % 2 == o))
-        def _():
-            finish(a)
-
-    new_log = old_log + factor + extra_in[0, 0:local, :] + extra_in[1, 0:local, :]
-    out_log[...] = new_log
-
     def onward(w, part, hop_to):
         spot = place(w, part)
         return remote(spot, spot, next_send.at[w, part], slot_recv.at[w, part], {"vec": hop_to})
@@ -527,15 +477,28 @@
         hop_to = jnp.where(side == 0, z + 1, z - 1)
         return w, away, hop_to
 
+    def forward(slots):
+        for a in slots:
+            for side in (near, 1 - near):
+                w, away, hop_to = route(side, a)
+
+                @pl.when(passes(a, away))
+                def _():
+                    for part in range(PARTS):
+                        onward(w, part, hop_to).wait_recv()
+                        onward(w, part, hop_to).start()
+
+    early = [a for a in range(half) if short and a < EARLY]
+    forward(early)
     for a in range(half):
-        for side in (near, 1 - near):
-            w, away, hop_to = route(side, a)
-
-            @pl.when(passes(a, away))
-            def _():
-                for part in range(PARTS):
-                    onward(w, part, hop_to).wait_recv()
-                    onward(w, part, hop_to).start()
+        @pl.when(at_owner[a] & (a % 2 == o))
+        def _():
+            finish(a)
+
+    new_log = old_log + factor + extra_in[0, 0:local, :] + extra_in[1, 0:local, :]
+    out_log[...] = new_log
+
+    forward([a for a in range(half) if a not in early])
 
     for copy in bias_copies:
         copy.wait_send()
@@ -567,12 +530,17 @@
     for a in range(half):
         @pl.when(at_owner[a])
         def _():
-            for hop in hops:
-                stage_copy(hop, a).wait_send()
+            def moved(n):
+                run = gathered.at[pl.ds(0, n)]
+                return remote(run, run, stage_send.at[a], slot_recv.at[0, 0], {"orb": 1 - o})
+
+            @pl.when(a % 2 == o)
+            def _():
+                moved(width - 1).wait_send()
 
             @pl.when(a % 2 != o)
             def _():
-                stage_copy(0, a).wait_send()
+                moved(width).wait_send()
 
                 whole = pl.ds(a * each, each)
                 remote(
@@ -591,8 +559,8 @@
     for a in range(half):
         @pl.when(at_owner[a] & (a % 2 == o))
         def _():
-            for copy in spread_copies(a):
-                copy.wait_send()
+            run = gathered.at[pl.ds(0, 2 * len(plans[a]) + 1)]
+            remote(run, run, own_send.at[a // 2], slot_recv.at[0, 0], {"orb": 1 - o}).wait_send()
             pltpu.make_async_copy(result.at[a // 2, o], gathered.at[base + a], write_sems.at[a // 2]).wait()
 
     for a in range(half):
@@ -616,7 +584,6 @@
     chunks = half * BLOCKS * SUB
     mine = half // 2
     lanes = 128
-    reach = max(max(depth - 1, 1) if depth - 1 <= REACH else 1, 2)
     dma = pltpu.SemaphoreType.DMA
     anywhere = pl.BlockSpec(memory_space=pl.ANY)
     out, out_log = pl.pallas_call(
@@ -639,10 +606,10 @@
             pltpu.VMEM((count, rows, electrons), BF16),
             pltpu.VMEM((block // span, wide, BLOCKS * block), BF16),
             pltpu.VMEM((wide, block), BF16),
-            pltpu.VMEM((2, width, local, wide), F32),
+            pltpu.VMEM((2, width, local, lanes), F32),
             pltpu.VMEM((width, local, lanes), F32),
             pltpu.VMEM((local, lanes), F32),
-            pltpu.VMEM((local, wide), F32),
+            pltpu.VMEM((local, lanes), F32),
             pltpu.VMEM((local, BLOCKS, block, block), F32),
             pltpu.VMEM((2, chunks, piece, block), BF16),
             pltpu.VMEM((2, chunks, piece, block), BF16),
@@ -673,9 +640,9 @@
             dma((2,)),
             dma((2,)),
             dma((2,)),
-            dma((width, half)),
-            dma((width, mine, 2)),
-            dma((mine, 2 * reach + 1, PARTS)),
+            dma((half,)),
+            dma((mine,)),
+            dma((mine,)),
             dma((local, PARTS)),
             dma((local, PARTS)),
             dma((mine,)),

time: 39.4 us -> 39.1 us (level)
  no operation moved by 1% of the time
where the time goes in v8:
time: 39.1 us; the launch traced here: 38.4 us
  Pallas kernels  37.8 us (97%)
  between operations  0.64 us (2%)
    pallas_call x1, Pallas kernels, per_device(): pl.pallas_call(functools.partial(kernel, depth, width), out_shape=(pltpu....  37 us
    pallas_call x1, Pallas kernels, per_device(): pl.pallas_call(settle, out_shape=(jax.ShapeDtypeStruct(walkers.shape, BF1...  0.82 us

profile of v8, /device:TPU:0, one launch (start us, length us, event | category | flops | bytes accessed | tf_op | source)
XLA Modules:
  0.0 38.4 jit_solution(6142698318163254022)
XLA Ops:
  0.6 37.0 %shard_map.86 = (bf16[8,256,128]{2,1,0:T(8,128)(2,1)S(1)}, f32[8,128]{1,0:T(8,128)S(1)}) custom-call(bf16[8,256,128]{2,1,0:T(8,128)(2,1)} %walkers_in.1, bf16[8,128,128]{2,1,0:T(8,128)(2,1)} %inverse_in.1, bf16[512,128]{1,0:T(8,128)(2,1)} %trial_in.1, bf16[8,256,512]{2,1,0:T(8,128)(2,1)} %vectors_in.1, f32[8,8]{1,0:T(8,128)} %aux_in.1, f32[8]{0:T(128)} %log_in.1, ...), custom_call_target="tpu_custom_call" | custom-call | tf_op jit(solution)/shard_map/pallas_call | solution.py:589
  37.6 0.8 %shard_map.87 = (bf16[8,256,128]{2,1,0:T(8,128)(2,1)}, f32[8]{0:T(128)}) custom-call(bf16[8,256,128]{2,1,0:T(8,128)(2,1)S(1)} %get-tuple-element.4.out_ref, f32[8,128]{1,0:T(8,128)S(1)} %get-tuple-element.5.log_ref), custom_call_target="tpu_custom_call" | custom-call | tf_op jit(solution)/shard_map/pallas_call | solution.py:663

commit v9 on v8

--- a/solution.py
+++ b/solution.py
@@ -205,12 +205,6 @@
     spread = jnp.broadcast_to(weighted.astype(F32)[:, None, :], (local, span, wide)).reshape(local * span, wide)
     kron = jnp.where(same, spread, 0.0).astype(BF16)
 
-    for j in range(block // span):
-        summed = jnp.dot(kron, strips[j], preferred_element_type=F32)
-        for n in range(BLOCKS):
-            partial[:, n, j * span:(j + 1) * span, :] = summed[:, n * block:(n + 1) * block].reshape(local, span, block)
-    edge_part = jnp.dot(weighted, level[...], preferred_element_type=F32)
-
     def to_next(side):
         return jnp.where(side == 0, z - 1, z + 1)
 
@@ -252,6 +246,34 @@
     def part_of(side, c):
         at = c % each
         return partial[side * half + c // each, at // SUB, pl.ds(pl.multiple_of((at % SUB) * piece, piece), piece), :]
+
+    def pass_on(side, c, togo):
+        here = (c // each) % 2 == o
+
+        @pl.when((togo > 1) | here)
+        def _():
+            chain_copy(side, c).start()
+
+        @pl.when((togo == 1) & jnp.logical_not(here))
+        def _():
+            cross_copy(side, c).start()
+
+    pair = BLOCKS // 2
+    ahead = pair * SUB
+    for n0 in range(0, BLOCKS, pair):
+        for j in range(block // span):
+            summed = jnp.dot(kron, strips[j, :, n0 * block:(n0 + pair) * block], preferred_element_type=F32)
+            for n in range(pair):
+                partial[:, n0 + n, j * span:(j + 1) * span, :] = summed[:, n * block:(n + 1) * block].reshape(
+                    local, span, block
+                )
+        if n0 == 0:
+            @pl.when(at_end)
+            def _():
+                for c in range(ahead):
+                    leaving[1 - near, c] = part_of(1 - near, c).astype(BF16)
+                    pass_on(1 - near, c, last - insets[0])
+    edge_part = jnp.dot(weighted, level[...], preferred_element_type=F32)
 
     def chain_step(t, carry):
         for turn in range(2):
@@ -262,10 +284,9 @@
             head = before == 0
             togo = after - depth_of(c)
 
-            @pl.when((c >= 0) & (c < chunks) & (togo > 0))
+            @pl.when((c >= jnp.where(head, ahead, 0)) & (c < chunks) & (togo > 0))
             def _():
                 own = part_of(side, c)
-                here = (c // each) % 2 == o
 
                 @pl.when(head)
                 def _():
@@ -276,13 +297,7 @@
                     chain_copy(side, c).wait_recv()
                     leaving[side, c] = (own + arrived[side, c].astype(F32)).astype(BF16)
 
-                @pl.when((togo > 1) | here)
-                def _():
-                    chain_copy(side, c).start()
-
-                @pl.when((togo == 1) & jnp.logical_not(here))
-                def _():
-                    cross_copy(side, c).start()
+                pass_on(side, c, togo)
 
             @pl.when((c == 0) & (after > 0))
             def _():

time: 39.1 us -> 38.9 us (level)
  no operation moved by 1% of the time
where the time goes in v9:
time: 38.9 us; the launch traced here: 38.3 us
  Pallas kernels  37.7 us (97%)
  between operations  0.64 us (2%)
    pallas_call x1, Pallas kernels, per_device(): pl.pallas_call(functools.partial(kernel, depth, width), out_shape=(pltpu....  36.8 us
    pallas_call x1, Pallas kernels, per_device(): pl.pallas_call(settle, out_shape=(jax.ShapeDtypeStruct(walkers.shape, BF1...  0.82 us

profile of v9, /device:TPU:0, one launch (start us, length us, event | category | flops | bytes accessed | tf_op | source)
XLA Modules:
  0.0 38.3 jit_solution(9026720999196734256)
XLA Ops:
  0.6 36.8 %shard_map.86 = (bf16[8,256,128]{2,1,0:T(8,128)(2,1)S(1)}, f32[8,128]{1,0:T(8,128)S(1)}) custom-call(bf16[8,256,128]{2,1,0:T(8,128)(2,1)} %walkers_in.1, bf16[8,128,128]{2,1,0:T(8,128)(2,1)} %inverse_in.1, bf16[512,128]{1,0:T(8,128)(2,1)} %trial_in.1, bf16[8,256,512]{2,1,0:T(8,128)(2,1)} %vectors_in.1, f32[8,8]{1,0:T(8,128)} %aux_in.1, f32[8]{0:T(128)} %log_in.1, ...), custom_call_target="tpu_custom_call" | custom-call | tf_op jit(solution)/shard_map/pallas_call | solution.py:604
  37.5 0.8 %shard_map.87 = (bf16[8,256,128]{2,1,0:T(8,128)(2,1)}, f32[8]{0:T(128)}) custom-call(bf16[8,256,128]{2,1,0:T(8,128)(2,1)S(1)} %get-tuple-element.4.out_ref, f32[8,128]{1,0:T(8,128)S(1)} %get-tuple-element.5.log_ref), custom_call_target="tpu_custom_call" | custom-call | tf_op jit(solution)/shard_map/pallas_call | solution.py:678

commit v10 on v9

--- a/solution.py
+++ b/solution.py
@@ -11,7 +11,7 @@
 ORDER = 6
 BLOCKS = 4
 SUB = 1
-SKEW = 4
+SKEW = 5
 EARLY = 1
 PARTS = 1
 LOADS = 2
@@ -315,8 +315,6 @@
 
         return carry
 
-    lax.fori_loop(0, SKEW * (last - 1) + chunks, chain_step, jnp.int32(0))
-
     for hop in hops:
         copies_copy(hop, lax.rem(x + hop, width)).wait_recv()
 
@@ -329,7 +327,7 @@
     def swap_core():
         return remote(edge.at[o], edge.at[o], edge_sems.at[0], edge_sems.at[1], {"orb": 1 - o})
 
-    for a in range(half):
+    def prepare(a):
         @pl.when(at_owner[a])
         def _():
             for hop in range(width):
@@ -357,15 +355,27 @@
 
                 lax.fori_loop(a * each, (a + 1) * each, give, jnp.int32(0))
 
+    def send_back(a):
+        @pl.when(at_end)
+        def _():
+            def back_step(c, carry):
+                leaving[near, c] = part_of(near, c).astype(BF16)
+                back_copy(c).start()
+                return carry
+
+            lax.fori_loop(a * each, (a + 1) * each, back_step, jnp.int32(0))
+
+    for a in range(half):
         if insets[a]:
-            @pl.when(at_end)
-            def _():
-                def back_step(c, carry):
-                    leaving[near, c] = part_of(near, c).astype(BF16)
-                    back_copy(c).start()
-                    return carry
-
-                lax.fori_loop(a * each, (a + 1) * each, back_step, jnp.int32(0))
+            prepare(a)
+
+    lax.fori_loop(0, SKEW * (last - 1) + chunks, chain_step, jnp.int32(0))
+
+    for a in range(half):
+        if not insets[a]:
+            prepare(a)
+        else:
+            send_back(a)
 
     for side in range(2):
         @pl.when(at_end & (near == side))

time: 38.9 us -> 38.7 us (level)
  no operation moved by 1% of the time
where the time goes in v10:
time: 38.7 us; the launch traced here: 38.3 us
  Pallas kernels  37.7 us (97%)
  between operations  0.64 us (2%)
    pallas_call x1, Pallas kernels, per_device(): pl.pallas_call(functools.partial(kernel, depth, width), out_shape=(pltpu....  36.8 us
    pallas_call x1, Pallas kernels, per_device(): pl.pallas_call(settle, out_shape=(jax.ShapeDtypeStruct(walkers.shape, BF1...  0.82 us

profile of v10, /device:TPU:0, one launch (start us, length us, event | category | flops | bytes accessed | tf_op | source)
XLA Modules:
  0.0 38.3 jit_solution(3814247628239518539)
XLA Ops:
  0.6 36.8 %shard_map.86 = (bf16[8,256,128]{2,1,0:T(8,128)(2,1)S(1)}, f32[8,128]{1,0:T(8,128)S(1)}) custom-call(bf16[8,256,128]{2,1,0:T(8,128)(2,1)} %walkers_in.1, bf16[8,128,128]{2,1,0:T(8,128)(2,1)} %inverse_in.1, bf16[512,128]{1,0:T(8,128)(2,1)} %trial_in.1, bf16[8,256,512]{2,1,0:T(8,128)(2,1)} %vectors_in.1, f32[8,8]{1,0:T(8,128)} %aux_in.1, f32[8]{0:T(128)} %log_in.1, ...), custom_call_target="tpu_custom_call" | custom-call | tf_op jit(solution)/shard_map/pallas_call | solution.py:614
  37.5 0.8 %shard_map.87 = (bf16[8,256,128]{2,1,0:T(8,128)(2,1)}, f32[8]{0:T(128)}) custom-call(bf16[8,256,128]{2,1,0:T(8,128)(2,1)S(1)} %get-tuple-element.4.out_ref, f32[8,128]{1,0:T(8,128)S(1)} %get-tuple-element.5.log_ref), custom_call_target="tpu_custom_call" | custom-call | tf_op jit(solution)/shard_map/pallas_call | solution.py:688

commit v11 on v10

--- a/solution.py
+++ b/solution.py
@@ -131,7 +131,7 @@
 
     bias_peers = [{"walk": lax.rem(x + hop, width), "orb": core} for hop in hops for core in range(2)] + [{"orb": 1 - o}]
     bias_copies = [
-        remote(bias_all.at[o, x], bias_all.at[o, x], bias_send.at[n], bias_recv.at[o, x], where)
+        remote(bias_all.at[o, x], bias_all.at[o, x], bias_send.at[0], bias_recv.at[0], where)
         for n, where in enumerate(bias_peers)
     ]
     def facts_copy(hop, owner):
@@ -182,13 +182,9 @@
     drawn = jnp.dot(known[:, 0:count], pick, precision=lax.Precision.HIGHEST, preferred_element_type=F32)
     old_log = jnp.broadcast_to(known[:, count:count + 1], (local, lanes))
 
-    for hop in hops:
-        other = lax.rem(x + hop, width)
-        for core in range(2):
-            remote(
-                bias_all.at[core, other], bias_all.at[core, other], bias_send.at[0], bias_recv.at[core, other], {"walk": other}
-            ).wait_recv()
-    remote(bias_all.at[1 - o, x], bias_all.at[1 - o, x], bias_send.at[0], bias_recv.at[1 - o, x], {"orb": 1 - o}).wait_recv()
+    tables = partial.at[0, 0, pl.ds(0, (2 * width - 1) * local)]
+    bias_done = remote(tables, tables, bias_send.at[0], bias_recv.at[0], {"orb": 1 - o})
+    bias_done.wait_recv()
 
     for s, (column, row) in enumerate(sources):
         picked[s:s + 1, :] = bias_all[0, column, row, :] + bias_all[1, column, row, :]
@@ -494,7 +490,7 @@
 
     def onward(w, part, hop_to):
         spot = place(w, part)
-        return remote(spot, spot, next_send.at[w, part], slot_recv.at[w, part], {"vec": hop_to})
+        return remote(spot, spot, next_send.at[w % half if short else w, part], slot_recv.at[w, part], {"vec": hop_to})
 
     def route(side, a):
         w = side * half + a
@@ -525,8 +521,7 @@
 
     forward([a for a in range(half) if a not in early])
 
-    for copy in bias_copies:
-        copy.wait_send()
+    bias_done.wait_send()
     for hop in hops:
         facts_copy(hop, x).wait_send()
         copies_copy(hop, x).wait_send()
@@ -654,8 +649,8 @@
             dma((width,)),
             dma((width,)),
             dma((width,)),
-            dma((2 * width,)),
-            dma((2, width)),
+            dma((1,)),
+            dma((1,)),
             dma((2, half)),
             dma((2, chunks)),
             dma((chunks // 2,)),
@@ -668,7 +663,7 @@
             dma((half,)),
             dma((mine,)),
             dma((mine,)),
-            dma((local, PARTS)),
+            dma((half if depth - 1 <= REACH else local, PARTS)),
             dma((local, PARTS)),
             dma((mine,)),
         ],

time: 38.7 us -> 38.6 us (level)
  no operation moved by 1% of the time
where the time goes in v11:
time: 38.6 us; the launch traced here: 38.2 us
  Pallas kernels  37.6 us (97%)
  between operations  0.64 us (2%)
    pallas_call x1, Pallas kernels, per_device(): pl.pallas_call(functools.partial(kernel, depth, width), out_shape=(pltpu....  36.8 us
    pallas_call x1, Pallas kernels, per_device(): pl.pallas_call(settle, out_shape=(jax.ShapeDtypeStruct(walkers.shape, BF1...  0.82 us

profile of v11, /device:TPU:0, one launch (start us, length us, event | category | flops | bytes accessed | tf_op | source)
XLA Modules:
  0.0 38.2 jit_solution(9069361112834888727)
XLA Ops:
  0.6 36.8 %shard_map.86 = (bf16[8,256,128]{2,1,0:T(8,128)(2,1)S(1)}, f32[8,128]{1,0:T(8,128)S(1)}) custom-call(bf16[8,256,128]{2,1,0:T(8,128)(2,1)} %walkers_in.1, bf16[8,128,128]{2,1,0:T(8,128)(2,1)} %inverse_in.1, bf16[512,128]{1,0:T(8,128)(2,1)} %trial_in.1, bf16[8,256,512]{2,1,0:T(8,128)(2,1)} %vectors_in.1, f32[8,8]{1,0:T(8,128)} %aux_in.1, f32[8]{0:T(128)} %log_in.1, ...), custom_call_target="tpu_custom_call" | custom-call | tf_op jit(solution)/shard_map/pallas_call | solution.py:609
  37.4 0.8 %shard_map.87 = (bf16[8,256,128]{2,1,0:T(8,128)(2,1)}, f32[8]{0:T(128)}) custom-call(bf16[8,256,128]{2,1,0:T(8,128)(2,1)S(1)} %get-tuple-element.4.out_ref, f32[8,128]{1,0:T(8,128)S(1)} %get-tuple-element.5.log_ref), custom_call_target="tpu_custom_call" | custom-call | tf_op jit(solution)/shard_map/pallas_call | solution.py:683

commit v12 on v10

--- a/solution.py
+++ b/solution.py
@@ -16,7 +16,7 @@
 PARTS = 1
 LOADS = 2
 REACH = 3
-PLANS = ((2, -1, 1), (3, 2, 1), (3, 2, 1), (2, 1))
+PLANS = ((2, -1, 1), (3, 2, 1), (3, 1), (2, 1))
 MESH = pl.DeviceIdType.MESH
 F32 = jnp.float32
 BF16 = jnp.bfloat16

time: 38.7 us -> 38.8 us (level)
  no operation moved by 1% of the time
where the time goes in v12:
time: 38.8 us; the launch traced here: 38.2 us
  Pallas kernels  37.6 us (97%)
  between operations  0.64 us (2%)
    pallas_call x1, Pallas kernels, per_device(): pl.pallas_call(functools.partial(kernel, depth, width), out_shape=(pltpu....  36.8 us
    pallas_call x1, Pallas kernels, per_device(): pl.pallas_call(settle, out_shape=(jax.ShapeDtypeStruct(walkers.shape, BF1...  0.82 us

profile of v12, /device:TPU:0, one launch (start us, length us, event | category | flops | bytes accessed | tf_op | source)
XLA Modules:
  0.0 38.2 jit_solution(4976614349048506046)
XLA Ops:
  0.6 36.8 %shard_map.86 = (bf16[8,256,128]{2,1,0:T(8,128)(2,1)S(1)}, f32[8,128]{1,0:T(8,128)S(1)}) custom-call(bf16[8,256,128]{2,1,0:T(8,128)(2,1)} %walkers_in.1, bf16[8,128,128]{2,1,0:T(8,128)(2,1)} %inverse_in.1, bf16[512,128]{1,0:T(8,128)(2,1)} %trial_in.1, bf16[8,256,512]{2,1,0:T(8,128)(2,1)} %vectors_in.1, f32[8,8]{1,0:T(8,128)} %aux_in.1, f32[8]{0:T(128)} %log_in.1, ...), custom_call_target="tpu_custom_call" | custom-call | tf_op jit(solution)/shard_map/pallas_call | solution.py:614
  37.4 0.8 %shard_map.87 = (bf16[8,256,128]{2,1,0:T(8,128)(2,1)}, f32[8]{0:T(128)}) custom-call(bf16[8,256,128]{2,1,0:T(8,128)(2,1)S(1)} %get-tuple-element.4.out_ref, f32[8,128]{1,0:T(8,128)S(1)} %get-tuple-element.5.log_ref), custom_call_target="tpu_custom_call" | custom-call | tf_op jit(solution)/shard_map/pallas_call | solution.py:688
